TPU v7x, 128 devices: a whole 4x4x4 slice. The times are simulated.
128 devices in a mesh: frames: 16 (over z, y_lo, core), heads: 8 (over x, y_hi).
Axes of the slice: x: 4, y: 4 (y_hi: 2, y_lo: 2; y = y_hi * 2 + y_lo), z: 4, core: 2. Of those that a mesh axis runs over, the one named last changes fastest.
Arguments:
- clip: bfloat16 [32, 16, 128, 320], P('frames', 'heads'), may hold values from -6 to 6
- w_time: bfloat16 [3, 320, 320], replicated, may hold values from -0.1875 to 0.1875
- w_down: bfloat16 [320, 1280], replicated, may hold values from -0.3125 to 0.3125
- w_embed: bfloat16 [320, 1280], replicated, may hold values from -0.3125 to 0.3125
- w_qkv: bfloat16 [1280, 3840], P(None, 'heads'), may hold values from -0.15625 to 0.15625
- w_out: bfloat16 [1280, 1280], P('heads'), may hold values from -0.15625 to 0.15625
- w_up: bfloat16 [1280, 320], replicated, may hold values from -0.15625 to 0.15625
- timestep: int32 [1], replicated, may hold values from 0 to 999
- cotangent: bfloat16 [32, 16, 128, 320], P('frames', 'heads'), may hold values from -6 to 6
Outputs:
- output: bfloat16 [32, 16, 128, 320], P('frames', 'heads')
- grad_clip: float32 [32, 16, 128, 320], P('frames', 'heads')
- grad_time: float32 [3, 320, 320], replicated
- grad_down: float32 [320, 1280], replicated
- grad_embed: float32 [320, 1280], replicated
- grad_qkv: float32 [1280, 3840], P(None, 'heads')
- grad_out: float32 [1280, 1280], P('heads')
- grad_up: float32 [1280, 320], replicated
All inputs are finite; a program needn't handle non-finite values.
Results may differ from a plain program's by a relative error of at most 0.024.
Values may be sent and summed in bfloat16 or wider, within the bound.
A program may use at most 128 MiB of HBM per device.

v0:
```python
import functools
import math

import jax
import jax.numpy as jnp
from jax import lax
from jax.experimental import pallas as pl
from jax.experimental.pallas import tpu as pltpu
from jax.sharding import PartitionSpec as P

HD = 80
MESH = pl.DeviceIdType.MESH
BF = jnp.bfloat16
F32 = jnp.float32
SCALE = 1.0 / math.sqrt(HD)
C = 320
CA = 384
CC = 1280
FPR = 1024


def mm(a, b):
    return jnp.dot(a, b, preferred_element_type=F32)


def mm_t0(a, b):
    return lax.dot_general(a, b, (((0,), (0,)), ((), ())), preferred_element_type=F32)


def mm_t1(a, b):
    return lax.dot_general(a, b, (((1,), (1,)), ((), ())), preferred_element_type=F32)


def iota(shape, dim):
    return lax.broadcasted_iota(jnp.int32, shape, dim)


def ones_where(cond):
    return jnp.where(cond, 1.0, 0.0).astype(BF)


def eye(n):
    return ones_where(iota((n, n), 0) == iota((n, n), 1))


def time_embed(timestep, width):
    half = width // 2
    freqs = jnp.exp(-math.log(10000.0) * jnp.arange(half, dtype=jnp.float32) / half)
    angle = timestep.astype(jnp.float32)[0] * freqs
    return jax.nn.silu(jnp.concatenate([jnp.cos(angle), jnp.sin(angle)])).astype(jnp.bfloat16)


class Sizes:
    def __init__(self, nf, nh, cols):
        self.nf, self.nh, self.cols = nf, nh, cols
        self.nc = nf // 2
        self.cells = 2 * cols
        self.tok = 4 * nf
        self.fr = FPR // nf
        self.yr = 2 * CC // nf
        self.ch = 32 if nh == 8 else self.yr // nh
        self.na = self.yr // self.ch


def main_kernel(
    z, clip, w_time, w_down, w_embed, w_qkv, w_out, w_up, embed, cot,
    out, grad_clip, fp_full, y_full, tap_full, w_aug,
    clip_l, clip_r, hidden, hg, hg_l, hg_r, acc,
    w_qkvp, w2, mh, wdu, w_out_t, w_aug_t,
    p_send, g_send, p_got, g_got, p_all, g_all, dg_all, att_all,
    ls_send, ls_got, slab_send, slab_got,
    fp, fp_pair, fp_sum, fp_got, tp, tp_pair, tp_sum, tp_got, tp_h, tp_hgot,
    y_send, y_got,
    halo_s, halo_r, hgs, hgr, a2a_s, a2a_r, ag_s, ag_r, rs_s, rs_r, sl_s, sl_r,
    pair_s, pair_r, fr_s, fr_r, ff_s, ff_r, fw_s, fw_r,
    th_s, th_r, ys_s, ys_r, yh_s, yh_r, yf_s, yf_r, yw_s, yw_r,
):
    nf, nh, nc = z.nf, z.nh, z.nc
    f, h = lax.axis_index("frames"), lax.axis_index("heads")
    chip, core = f // 2, lax.rem(f, 2)
    partner = chip * 2 + 1 - core

    def send(src, dst, ssem, rsem, to):
        copy = pltpu.make_async_remote_copy(
            src_ref=src, dst_ref=dst, send_sem=ssem, recv_sem=rsem, device_id=to, device_id_type=MESH
        )
        copy.start()

    def wait_send(src, sem):
        pltpu.make_async_remote_copy(
            src_ref=src, dst_ref=src, send_sem=sem, recv_sem=sem, device_id=(f, h), device_id_type=MESH
        ).wait_send()

    def wait_recv(dst, sem):
        pltpu.make_async_remote_copy(
            src_ref=dst, dst_ref=dst, send_sem=sem, recv_sem=sem, device_id=(f, h), device_id_type=MESH
        ).wait_recv()

    def other_f(k):
        return lax.rem(f + k, nf)

    def other_h(k):
        return lax.rem(h + k, nh)

    def other_c(k):
        return lax.rem(chip + k, nc)

    barrier = pltpu.get_barrier_semaphore()
    for k in range(1, nf):
        pl.semaphore_signal(barrier, inc=1, device_id=(other_f(k), h), device_id_type=MESH)
    for k in range(1, nh):
        pl.semaphore_signal(barrier, inc=1, device_id=(f, other_h(k)), device_id_type=MESH)
    pl.semaphore_wait(barrier, nf + nh - 2)

    @pl.when(f > 0)
    def _():
        send(clip.at[0], clip_r, halo_s.at[0], halo_r.at[0], (f - 1, h))

    @pl.when(f < nf - 1)
    def _():
        send(clip.at[1], clip_l, halo_s.at[1], halo_r.at[1], (f + 1, h))

    srow, scell = iota((8 * nf, z.cells), 0), iota((8 * nf, z.cells), 1)
    spos, sp = (srow // 8) * 4, lax.rem(srow, 8)
    column = lax.rem(scell, z.cols) // 2
    pool_p = ones_where((sp < 4) & (spos + sp == column))
    pool_g = ones_where((sp >= 4) & (spos + sp - 4 == column))
    g_slab = mm(pool_g, cot[0]) + mm(pool_g, cot[1])
    g_send[...] = jnp.zeros_like(g_send)
    g_send[:, :, 0:C] = g_slab.reshape(nf, 8, C).astype(BF)
    for k in range(1, nf):
        to = other_f(k)
        send(g_send.at[to], g_got.at[f], a2a_s.at[0, to], a2a_r.at[0, f], (to, h))
    g_got[f] = g_send[f]

    acc[0] = mm(clip[0], w_time[1]) + mm(clip[1], w_time[2])
    acc[1] = mm(clip[0], w_time[0]) + mm(clip[1], w_time[1])

    sel_rows, sel_cols = iota((z.tok, 8 * nf), 0), iota((z.tok, 8 * nf), 1)
    want = (sel_rows // 4) * 8 + lax.rem(sel_rows, 4)
    sel_p = ones_where(sel_cols == want)
    sel_g = ones_where(sel_cols == want + 4)

    for k in range(1, nf):
        fr = other_f(k)
        wait_recv(g_got.at[fr], a2a_r.at[0, fr])
    g_all[h] = mm(sel_g, g_got[...].astype(F32).reshape(8 * nf, CA).astype(BF)).astype(BF)
    for k in range(1, nh):
        to = other_h(k)
        send(g_all.at[h], g_all.at[h], ag_s.at[0, to], ag_r.at[0, h], (f, to))

    @pl.when(f > 0)
    def _():
        wait_recv(clip_l, halo_r.at[1])

    @pl.when(f == 0)
    def _():
        clip_l[...] = jnp.zeros_like(clip_l)

    @pl.when(f < nf - 1)
    def _():
        wait_recv(clip_r, halo_r.at[0])

    @pl.when(f == nf - 1)
    def _():
        clip_r[...] = jnp.zeros_like(clip_r)

    hidden[0] = (clip[0].astype(F32) + acc[0] + mm(clip_l[...], w_time[0])).astype(BF)
    hidden[1] = (clip[1].astype(F32) + acc[1] + mm(clip_r[...], w_time[2])).astype(BF)
    p_slab = (mm(pool_p, hidden[0]) + mm(pool_p, hidden[1])) * 0.125
    lane, prow = iota((nf, 8, CA), 2), iota((nf, 8, CA), 1)
    p_send[...] = ones_where((lane == C) & (prow < 4))
    p_send[:, :, 0:C] = p_slab.reshape(nf, 8, C).astype(BF)
    for k in range(1, nf):
        to = other_f(k)
        send(p_send.at[to], p_got.at[f], a2a_s.at[1, to], a2a_r.at[1, f], (to, h))
    p_got[f] = p_send[f]

    shift = mm(embed[...], w_embed[...])
    w_aug[0:C] = w_down[...]
    w_aug[C:CA] = jnp.where(iota((CA - C, CC), 0) == 0, jnp.broadcast_to(shift[0:1], (CA - C, CC)), 0.0).astype(BF)
    wide_row, wide_col = iota((6 * HD, 768), 0), iota((6 * HD, 768), 1)
    spread_cols = ones_where((wide_row // HD == wide_col // 128) & (lax.rem(wide_row, HD) == lax.rem(wide_col, 128)))
    w_qkvp[...] = mm(w_qkv[...], spread_cols).astype(BF)
    w2[...] = mm(w_aug[...], w_qkvp[...]).astype(BF)
    mix = mm(w_out[...], w_up[...]).astype(BF)
    mh[...] = jnp.zeros_like(mh)
    mh[0:HD, 0:C] = mix[0:HD]
    mh[128 : 128 + HD, 0:C] = mix[HD : 2 * HD]
    wdu[...] = jnp.zeros_like(wdu)
    wdu[:, 0:C] = mm(w_aug[...], w_up[...]).astype(BF)

    for k in range(1, nf):
        fr = other_f(k)
        wait_recv(p_got.at[fr], a2a_r.at[1, fr])
    p_all[h] = mm(sel_p, p_got[...].astype(F32).reshape(8 * nf, CA).astype(BF)).astype(BF)
    for k in range(1, nh):
        to = other_h(k)
        send(p_all.at[h], p_all.at[h], ag_s.at[1, to], ag_r.at[1, h], (f, to))

    w_out_t[...] = mm_t0(w_out[...], eye(2 * HD)).astype(BF)
    w_aug_t[...] = mm_t0(w_aug[...], eye(CA)).astype(BF)

    for k in range(1, nh):
        fr = other_h(k)
        wait_recv(g_all.at[fr], ag_r.at[0, fr])
        wait_recv(p_all.at[fr], ag_r.at[1, fr])

    bt = 2 * z.tok
    arow, acol = iota((bt, bt), 0), iota((bt, bt), 1)
    mask = (arow // z.tok == acol // z.tok) & (lax.rem(arow, 4) == lax.rem(acol, 4))

    def block(b, carry):
        two = pl.ds(2 * b, 2)
        rows = pl.ds(pl.multiple_of(b * bt, bt), bt)
        pb = p_all[two].reshape(bt, CA)
        gb = g_all[two].reshape(bt, CA)
        qkv = mm(pb, w2[...]).astype(BF)
        ag = mm_t1(gb, mh[...]).astype(BF)
        grads, atts = [], []
        for n in range(2):
            q, k, v = (qkv[:, (3 * n + i) * 128 : (3 * n + i + 1) * 128] for i in range(3))
            a = ag[:, n * 128 : (n + 1) * 128]
            scores = jnp.where(mask, mm_t1(q, k) * SCALE, -1e30)
            e = jnp.exp(scores - jnp.max(scores, axis=1, keepdims=True))
            probs = e / jnp.sum(e, axis=1, keepdims=True)
            weights = probs.astype(BF)
            atts.append(mm(weights, v).astype(BF))
            wg = mm_t1(a, v)
            sg = (probs * (wg - jnp.sum(probs * wg, axis=1, keepdims=True)) * SCALE).astype(BF)
            grads += [mm(sg, k).astype(BF), mm_t0(sg, q).astype(BF), mm_t0(weights, a).astype(BF)]
        dg = jnp.concatenate(grads, axis=1)
        att = jnp.concatenate(atts, axis=1)
        dg_all[rows] = dg
        att_all[rows] = att
        ls_send[two, :, 0:CA] = mm(att, mh[...]).astype(BF).reshape(2, z.tok, CA)
        ls_send[two, :, CA : 2 * CA] = mm_t1(dg, w2[...]).astype(BF).reshape(2, z.tok, CA)
        return carry

    lax.fori_loop(0, nh // 2, block, 0)

    for k in range(1, nh):
        to = other_h(k)
        send(ls_send.at[to], ls_got.at[h], rs_s.at[to], rs_r.at[h], (f, to))

    tokens = z.nh * z.tok
    p_mat, g_mat = p_all[...].reshape(tokens, CA), g_all[...].reshape(tokens, CA)
    r_pad = mm_t0(dg_all[...], p_mat)
    a_pad = mm_t0(att_all[...], g_mat)
    x_pad = mm_t0(g_mat, p_mat)
    rows_of = [r_pad[128 * i : 128 * i + HD] for i in range(6)] + [a_pad[0:HD], a_pad[128 : 128 + HD]]
    sums = jnp.concatenate(rows_of + [x_pad[0:C], jnp.zeros((FPR - 960, CA), F32)], axis=0)
    fp[...] = sums.astype(BF).reshape(nc, 2, z.fr, CA)
    send(fp.at[:, 1 - core], fp_pair, pair_s.at[0], pair_r.at[0], (partner, h))

    def reduce_scatter(own, pair, total, got, n):
        wait_recv(pair, pair_r.at[n])
        total[...] = (own[:, core].astype(F32) + pair[...].astype(F32)).astype(BF)
        for k in range(1, nc):
            to = other_c(k)
            send(total.at[to], got.at[chip], fr_s.at[n, to], fr_r.at[n, chip], (to * 2 + core, h))

    def reduced(total, got, n):
        value = total[chip].astype(F32)
        for k in range(1, nc):
            fr = other_c(k)
            wait_recv(got.at[fr], fr_r.at[n, fr])
            value = value + got[fr].astype(F32)
        return value

    def gather_start(full, ssem, rsem):
        for k in range(1, nc):
            to = other_c(k)
            send(full.at[chip, core], full.at[chip, core], ssem.at[to], rsem.at[chip], (to * 2 + core, h))

    def gather_pass(full, rsem, wsem, wrsem):
        send(full.at[chip, core], full.at[chip, core], wsem.at[chip], wrsem.at[chip], (partner, h))
        for k in range(1, nc):
            fr = other_c(k)
            wait_recv(full.at[fr, core], rsem.at[fr])
            send(full.at[fr, core], full.at[fr, core], wsem.at[fr], wrsem.at[fr], (partner, h))

    def gather_end(full, wrsem):
        for k in range(nc):
            fr = other_c(k)
            wait_recv(full.at[fr, 1 - core], wrsem.at[fr])

    reduce_scatter(fp, fp_pair, fp_sum, fp_got, 0)

    ls = ls_send[h].astype(F32)
    for k in range(1, nh):
        fr = other_h(k)
        wait_recv(ls_got.at[fr], rs_r.at[fr])
        ls = ls + ls_got[fr].astype(F32)
    ls = ls.astype(BF)
    erow, ecol = iota((8 * nf, z.tok), 0), iota((8 * nf, z.tok), 1)
    ep, et = lax.rem(erow, 8), (erow // 8) * 4
    put_l = ones_where((ep < 4) & (et + ep == ecol))
    put_s = ones_where((ep >= 4) & (et + ep - 4 == ecol))
    slab = mm(put_l, ls[:, 0:CA]) + mm(put_s, ls[:, CA : 2 * CA])
    slab_send[...] = slab.reshape(nf, 8, CA).astype(BF)
    for k in range(1, nf):
        to = other_f(k)
        send(slab_send.at[to], slab_got.at[f], sl_s.at[to], sl_r.at[f], (to, h))
    slab_got[f] = slab_send[f]

    local = mm(p_send[...].astype(F32).reshape(8 * nf, CA).astype(BF), wdu[...])
    local = local + mm_t1(g_send[...].astype(F32).reshape(8 * nf, CA).astype(BF), wdu[...])

    fp_full[chip, core] = reduced(fp_sum, fp_got, 0).astype(BF)
    gather_start(fp_full, ff_s.at[0], ff_r.at[0])

    for k in range(1, nf):
        fr = other_f(k)
        wait_recv(slab_got.at[fr], sl_r.at[fr])
    lsf = (slab_got[...].astype(F32).reshape(8 * nf, CA) + local).astype(BF)
    urow, ucol = iota((z.cells, 8 * nf), 0), iota((z.cells, 8 * nf), 1)
    upos = lax.rem(urow, z.cols) // 2
    ucell = (upos // 4) * 8 + lax.rem(upos, 4)
    up_l = ones_where(ucol == ucell)
    up_s = ones_where(ucol == ucell + 4)
    spread = mm(up_s, lsf)[:, 0:C] * 0.125
    hg[0] = (cot[0].astype(F32) + spread).astype(BF)
    hg[1] = (cot[1].astype(F32) + spread).astype(BF)

    @pl.when(f > 0)
    def _():
        send(hg.at[0], hg_r, hgs.at[0], hgr.at[0], (f - 1, h))

    @pl.when(f < nf - 1)
    def _():
        send(hg.at[1], hg_l, hgs.at[1], hgr.at[1], (f + 1, h))

    tap0 = mm_t0(clip_l[...], hg[0]) + mm_t0(clip[0], hg[1])
    tap1 = mm_t0(clip[0], hg[0]) + mm_t0(clip[1], hg[1])
    tap2 = mm_t0(clip[1], hg[0]) + mm_t0(clip_r[...], hg[1])
    taps = jnp.concatenate([tap0, tap1, tap2, jnp.zeros((FPR - 960, C), F32)], axis=0)
    tp[...] = jnp.zeros_like(tp)
    tp[:, :, :, 0:C] = taps.astype(BF).reshape(nc, 2, z.fr, C)
    send(tp.at[:, 1 - core], tp_pair, pair_s.at[1], pair_r.at[1], (partner, h))

    gather_pass(fp_full, ff_r.at[0], fw_s.at[0], fw_r.at[0])
    reduce_scatter(tp, tp_pair, tp_sum, tp_got, 1)
    lifted = mm(up_l, lsf)[:, 0:C]
    out[0] = (hidden[0].astype(F32) + lifted).astype(BF)
    out[1] = (hidden[1].astype(F32) + lifted).astype(BF)

    gather_end(fp_full, fw_r.at[0])
    whole = fp_full[...].reshape(FPR, CA)

    @pl.when(f < nf // 2)
    def _():
        rows = pl.ds(pl.multiple_of(f * z.yr, 32), z.yr)
        y_send[...] = mm(w_qkv[rows], whole[0:480]).astype(BF).reshape(z.na, z.ch, CA)

    @pl.when(f >= nf // 2)
    def _():
        rows = pl.ds(pl.multiple_of((f - nf // 2) * z.yr, 32), z.yr)
        y_send[...] = mm(w_out_t[rows], whole[480:640]).astype(BF).reshape(z.na, z.ch, CA)

    for j in range(z.na):

        @pl.when(h != j)
        def _():
            send(y_send.at[j], y_got.at[h], ys_s.at[j], ys_r.at[h], (f, j))

    tp_h[...] = reduced(tp_sum, tp_got, 1).astype(BF)
    for k in range(1, nh):
        to = other_h(k)
        send(tp_h, tp_hgot.at[h], th_s.at[to], th_r.at[h], (f, to))

    @pl.when(h < z.na)
    def _():
        value = y_send[h].astype(F32)
        for k in range(1, nh):
            fr = other_h(k)
            wait_recv(y_got.at[fr], ys_r.at[fr])
            value = value + y_got[fr].astype(F32)
        x_t = whole[640:960]

        @pl.when(f < nf // 2)
        def _():
            rows = pl.ds(pl.multiple_of(f * z.yr + h * z.ch, 32), z.ch)
            y_full[chip, core, h] = (value + mm(w_up[rows], x_t)).astype(BF)

        @pl.when(f >= nf // 2)
        def _():
            rows = pl.ds(pl.multiple_of((f - nf // 2) * z.yr + h * z.ch, 32), z.ch)
            x_part = mm_t1(w_aug_t[rows], x_t)
            y_full[chip, core, h] = value.astype(BF)
            y_full[chip, core, h, :, 0:C] = (value[:, 0:C] + x_part).astype(BF)

        for k in range(1, nh):
            to = other_h(k)
            send(y_full.at[chip, core, h], y_full.at[chip, core, h], yh_s.at[to], yh_r.at[h], (f, to))

    @pl.when(f > 0)
    def _():
        wait_recv(hg_l, hgr.at[1])

    @pl.when(f == 0)
    def _():
        hg_l[...] = jnp.zeros_like(hg_l)

    @pl.when(f < nf - 1)
    def _():
        wait_recv(hg_r, hgr.at[0])

    @pl.when(f == nf - 1)
    def _():
        hg_r[...] = jnp.zeros_like(hg_r)

    grad_clip[0] = (
        hg[0].astype(F32) + mm_t1(hg[1], w_time[0]) + mm_t1(hg[0], w_time[1]) + mm_t1(hg_l[...], w_time[2])
    )
    grad_clip[1] = (
        hg[1].astype(F32) + mm_t1(hg_r[...], w_time[0]) + mm_t1(hg[1], w_time[1]) + mm_t1(hg[0], w_time[2])
    )

    value = tp_h[...].astype(F32)
    for k in range(1, nh):
        fr = other_h(k)
        wait_recv(tp_hgot.at[fr], th_r.at[fr])
        value = value + tp_hgot[fr].astype(F32)
    tap_full[chip, core] = value.astype(BF)
    gather_start(tap_full, ff_s.at[1], ff_r.at[1])

    for j in range(z.na):

        @pl.when(h != j)
        def _():
            wait_recv(y_full.at[chip, core, j], yh_r.at[j])

    gather_start(y_full, yf_s, yf_r)
    gather_pass(tap_full, ff_r.at[1], fw_s.at[1], fw_r.at[1])
    gather_pass(y_full, yf_r, yw_s, yw_r)
    gather_end(tap_full, fw_r.at[1])
    gather_end(y_full, yw_r)

    @pl.when(f > 0)
    def _():
        wait_send(clip.at[0], halo_s.at[0])
        wait_send(hg.at[0], hgs.at[0])

    @pl.when(f < nf - 1)
    def _():
        wait_send(clip.at[1], halo_s.at[1])
        wait_send(hg.at[1], hgs.at[1])

    for k in range(1, nf):
        to = other_f(k)
        wait_send(g_send.at[to], a2a_s.at[0, to])
        wait_send(p_send.at[to], a2a_s.at[1, to])
        wait_send(slab_send.at[to], sl_s.at[to])
    for k in range(1, nh):
        to = other_h(k)
        wait_send(g_all.at[h], ag_s.at[0, to])
        wait_send(p_all.at[h], ag_s.at[1, to])
        wait_send(ls_send.at[to], rs_s.at[to])
        wait_send(tp_h, th_s.at[to])
    wait_send(fp_pair, pair_s.at[0])
    wait_send(tp_pair, pair_s.at[1])
    for k in range(1, nc):
        to = other_c(k)
        wait_send(fp_sum.at[to], fr_s.at[0, to])
        wait_send(tp_sum.at[to], fr_s.at[1, to])
        wait_send(fp_full.at[chip, core], ff_s.at[0, to])
        wait_send(tap_full.at[chip, core], ff_s.at[1, to])
        wait_send(y_full.at[chip, core], yf_s.at[to])
    for k in range(nc):
        to = other_c(k)
        wait_send(fp_full.at[to, core], fw_s.at[0, to])
        wait_send(tap_full.at[to, core], fw_s.at[1, to])
        wait_send(y_full.at[to, core], yw_s.at[to])
    for j in range(z.na):

        @pl.when(h != j)
        def _():
            wait_send(y_send.at[j], ys_s.at[j])

    @pl.when(h < z.na)
    def _():
        for k in range(1, nh):
            to = other_h(k)
            wait_send(y_full.at[chip, core, h], yh_s.at[to])


def final_kernel(
    fp_full, y_full, tap_full, w_aug, w_up, embed_col,
    grad_time, grad_down, grad_embed, grad_qkv, grad_out, grad_up,
):
    grad_time[...] = tap_full[0:960, 0:C].astype(F32)
    down = mm_t1(eye(CA), y_full[0:CC])
    grad_down[...] = down[0:C]
    grad_embed[...] = embed_col[...] * down[C : C + 1]
    grad_up[...] = y_full[CC : 2 * CC, 0:C].astype(F32)
    grad_qkv[...] = lax.dot_general(
        w_aug[...], fp_full[0:480], (((0,), (1,)), ((), ())), preferred_element_type=F32
    )
    grad_out[...] = mm_t1(fp_full[480:640, 0:C], w_up[...])


def shards(z, clip, w_time, w_down, w_embed, w_qkv, w_out, w_up, timestep, cotangent):
    nf, nh, nc = z.nf, z.nh, z.nc
    shape4 = clip.shape
    embed = time_embed(timestep, w_embed.shape[0])
    embed_rows = jnp.broadcast_to(embed[None, :], (16, C))
    vm = pl.BlockSpec(memory_space=pltpu.VMEM)
    dma = pltpu.SemaphoreType.DMA

    def bf(*shape):
        return pltpu.VMEM(shape, BF)

    frame = (z.cells, C)
    outs = pl.pallas_call(
        functools.partial(main_kernel, z),
        out_shape=(
            jax.ShapeDtypeStruct((2, *frame), BF),
            jax.ShapeDtypeStruct((2, *frame), F32),
            jax.ShapeDtypeStruct((nc, 2, z.fr, CA), BF),
            jax.ShapeDtypeStruct((nc, 2, z.na, z.ch, CA), BF),
            jax.ShapeDtypeStruct((nc, 2, z.fr, CA), BF),
            jax.ShapeDtypeStruct((CA, CC), BF),
        ),
        in_specs=[vm] * 9,
        out_specs=(vm,) * 6,
        scratch_shapes=[
            bf(*frame), bf(*frame), bf(2, *frame), bf(2, *frame), bf(*frame), bf(*frame),
            pltpu.VMEM((2, *frame), F32),
            bf(CC, 768), bf(CA, 768), bf(256, CA), bf(CA, CA), bf(CC, 2 * HD), bf(CC, CA),
            bf(nf, 8, CA), bf(nf, 8, CA), bf(nf, 8, CA), bf(nf, 8, CA),
            bf(nh, z.tok, CA), bf(nh, z.tok, CA), bf(nh * z.tok, 768), bf(nh * z.tok, 256),
            bf(nh, z.tok, 2 * CA), bf(nh, z.tok, 2 * CA), bf(nf, 8, CA), bf(nf, 8, CA),
            bf(nc, 2, z.fr, CA), bf(nc, z.fr, CA), bf(nc, z.fr, CA), bf(nc, z.fr, CA),
            bf(nc, 2, z.fr, CA), bf(nc, z.fr, CA), bf(nc, z.fr, CA), bf(nc, z.fr, CA),
            bf(z.fr, CA), bf(nh, z.fr, CA),
            bf(z.na, z.ch, CA), bf(nh, z.ch, CA),
            dma((2,)), dma((2,)), dma((2,)), dma((2,)),
            dma((2, nf)), dma((2, nf)), dma((2, nh)), dma((2, nh)),
            dma((nh,)), dma((nh,)), dma((nf,)), dma((nf,)),
            dma((2,)), dma((2,)), dma((2, nc)), dma((2, nc)),
            dma((2, nc)), dma((2, nc)), dma((2, nc)), dma((2, nc)),
            dma((nh,)), dma((nh,)), dma((nh,)), dma((nh,)),
            dma((nh,)), dma((nh,)), dma((nc,)), dma((nc,)), dma((nc,)), dma((nc,)),
        ],
        compiler_params=pltpu.CompilerParams(
            collective_id=0, has_side_effects=True, vmem_limit_bytes=60 * 1024 * 1024
        ),
    )(
        clip.reshape(2, *frame), w_time, w_down, w_embed, w_qkv, w_out, w_up, embed_rows,
        cotangent.reshape(2, *frame),
    )
    out, grad_clip, fp_full, y_full, tap_full, w_aug = outs
    grads = pl.pallas_call(
        final_kernel,
        out_shape=(
            jax.ShapeDtypeStruct((960, C), F32),
            jax.ShapeDtypeStruct((C, CC), F32),
            jax.ShapeDtypeStruct((C, CC), F32),
            jax.ShapeDtypeStruct((CC, 480), F32),
            jax.ShapeDtypeStruct((2 * HD, CC), F32),
            jax.ShapeDtypeStruct((CC, C), F32),
        ),
        in_specs=[vm] * 6,
        out_specs=(vm,) * 6,
        compiler_params=pltpu.CompilerParams(vmem_limit_bytes=48 * 1024 * 1024),
    )(
        fp_full.reshape(FPR, CA), y_full.reshape(2 * CC, CA), tap_full.reshape(FPR, CA),
        w_aug, w_up, embed.astype(F32)[:, None],
    )
    grad_time, grad_down, grad_embed, grad_qkv, grad_out, grad_up = grads
    return (
        out.reshape(shape4),
        grad_clip.reshape(shape4),
        grad_time.reshape(3, C, C),
        grad_down,
        grad_embed,
        grad_qkv,
        grad_out,
        grad_up,
    )


def solution(mesh, cols=128):
    z = Sizes(mesh.shape["frames"], mesh.shape["heads"], cols)
    return jax.shard_map(
        functools.partial(shards, z),
        mesh=mesh,
        in_specs=(
            P("frames", "heads", None, None),
            P(),
            P(),
            P(),
            P(None, "heads"),
            P("heads", None),
            P(),
            P(),
            P("frames", "heads", None, None),
        ),
        out_specs=(
            P("frames", "heads", None, None),
            P("frames", "heads", None, None),
            P(),
            P(),
            P(),
            P(None, "heads"),
            P("heads", None),
            P(),
        ),
        check_vma=False,
    )
```

profile of v0, /device:TPU:1, one launch (start us, length us, event | category | flops | bytes accessed | tf_op | source)
XLA Modules:
  0.0 129.5 jit_solution(10566957508523641823)
XLA Ops:
  0.6 0.0 copy-start.5
  1.4 0.1 fusion
  1.5 0.1 convert_convert_fusion
  1.6 0.6 broadcast_in_dim.2.embed
  2.2 0.1 copy.54.embed_col
  2.4 0.0 copy-start.4
  2.4 2.0 %copy.49 = bf16[2,2,128,320]{3,2,1,0:T(8,128)(2,1)} copy(bf16[2,2,128,320]{2,3,1,0:T(8,128)(2,1)} %param.9) | data formatting | bytes 655360 | tf_op args[0]
  4.4 1.9 %copy.50 = bf16[2,2,128,320]{3,2,1,0:T(8,128)(2,1)} copy(bf16[2,2,128,320]{2,3,1,0:T(8,128)(2,1)} %param.17) | data formatting | bytes 655360 | tf_op args[8]
  6.2 0.0 copy-done.5
  6.2 1.3 copy.52.w_up
  7.5 0.0 copy-done.4
  7.5 1.5 %copy.51.w_qkv = bf16[1280,480]{1,0:T(8,128)(2,1)} copy(bf16[1280,480]{0,1:T(8,128)(2,1)S(1)} %copy-done.4) | data formatting | bytes 2457600 | tf_op args[4]
  9.0 102.1 %shard_map.152 = (bf16[2,256,320]{2,1,0:T(8,128)(2,1)}, f32[2,256,320]{2,1,0:T(8,128)}, bf16[8,2,64,384]{3,2,1,0:T(8,128)(2,1)}, bf16[8,2,5,32,384]{4,3,2,1,0:T(...) custom-call(bf16[2,256,320]{2,1,0:T(8,128)(2,1)} %bitcast.14, bf16[3,320,320]{2,1,0:T(8,128)(2,1)} %w_time.1, ...), custom_call_target="tpu_custom_call" | custom-call | tf_op jit(solution)/shard_map/pallas_call | solution.py:515
  111.1 0.0 copy-start
  111.1 2.0 %copy.55 = bf16[2,2,128,320]{2,3,1,0:T(8,128)(2,1)} copy(bf16[2,2,128,320]{3,2,1,0:T(8,128)(2,1)} %bitcast.17) | data formatting | bytes 655360
  113.0 2.2 %copy.56 = f32[2,2,128,320]{2,3,1,0:T(8,128)} copy(f32[2,2,128,320]{3,2,1,0:T(8,128)} %bitcast.16) | data formatting | bytes 1310720
  115.3 0.0 copy-done
  115.3 0.0 copy-start.1
  115.3 1.2 copy-done.1
  116.5 1.1 copy-done.2
  117.6 1.1 copy-done.3
  118.8 5.9 %shard_map.153 = (f32[960,320]{1,0:T(8,128)}, f32[320,1280]{1,0:T(8,128)}, f32[320,1280]{1,0:T(8,128)}, f32[1280,480]{1,0:T(8,128)}, f32[160,1280]{1,0:T(8,128)}, /*index=5*/f32[1280,320]{1,0:T(8,128)S(1)}) custom-call(bf16[1024,384]{1,0:T(8,128)(2,1)S(1)} %bitcast.11, bf16[2560,384]{1,0:T(8,128)(2,1)} %bitcast.13, bf16[1024,384]{1,0:T(8,128)(2,1)S(1)} %bitcast.12, ...), custom_call_target="tpu_custom_call" | custom-call | tf_op jit(solution)/shard_map/pallas_call | solution.py:554
  124.7 1.7 %copy.58 = f32[1280,320]{0,1:T(8,128)} copy(f32[1280,320]{1,0:T(8,128)S(1)} %get-tuple-element.63) | data formatting | bytes 3276800
  126.3 3.1 %copy.57 = f32[1280,480]{0,1:T(8,128)} copy(f32[1280,480]{1,0:T(8,128)} %get-tuple-element.61) | data formatting | bytes 4915200
  (3 shorter events, 0.1 us)
Async XLA Ops:
  0.6 5.6 %copy-start.5 = (bf16[1280,320]{0,1:T(8,128)(2,1)S(1)}, bf16[1280,320]{0,1:T(8,128)(2,1)}, u32[]{:S(2)}) copy-start(bf16[1280,320]{0,1:T(8,128)(2,1)} %param.15) | copy-start | bytes 2457604
  2.4 5.2 %copy-start.4 = (bf16[1280,480]{0,1:T(8,128)(2,1)S(1)}, bf16[1280,480]{0,1:T(8,128)(2,1)}, u32[]{:S(2)}) copy-start(bf16[1280,480]{0,1:T(8,128)(2,1)} %param.13) | copy-start | bytes 3686404
  111.1 4.2 %copy-start = (bf16[1280,320]{1,0:T(8,128)(2,1)S(1)}, bf16[1280,320]{1,0:T(8,128)(2,1)}, u32[]{:S(2)}) copy-start(bf16[1280,320]{1,0:T(8,128)(2,1)} %copy.52.w_up) | copy-start | bytes 2457604
  115.3 1.2 copy-start.1
  116.5 1.1 copy-start.2
  117.6 1.1 copy-start.3
where the time goes:
time: 130 us; the launch traced here: 129 us
  Pallas kernels  108 us (83%)
  local copies, waits for them, and re-layouts  19.9 us (15%)
  between operations  1.41 us (1%)
    pallas_call x1, Pallas kernels, shards(): pl.pallas_call(functools.partial(main_kernel, z), out_shape=(jax.ShapeDty...  102 us
    unnamed x20, local copies, waits for them, and re-layouts  19.1 us
    pallas_call x1, Pallas kernels, shards(): pl.pallas_call(final_kernel, out_shape=(jax.ShapeDtypeStruct((960, C), F3...  5.9 us

commit v1 on v0

v1 whole, which is shorter than its diff:
```python
import functools
import math

import jax
import jax.numpy as jnp
from jax import lax
from jax.experimental import pallas as pl
from jax.experimental.pallas import tpu as pltpu
from jax.sharding import PartitionSpec as P

HD = 80
MESH = pl.DeviceIdType.MESH
BF = jnp.bfloat16
F32 = jnp.float32
SCALE = 1.0 / math.sqrt(HD)
C = 320
CA = 384
CC = 1280
LW = 2 * C
RAW = 8 * HD
FPW = RAW + 2 * CA


def mm(a, b):
    return jnp.dot(a, b, preferred_element_type=F32)


def mm_t0(a, b):
    return lax.dot_general(a, b, (((0,), (0,)), ((), ())), preferred_element_type=F32)


def mm_t1(a, b):
    return lax.dot_general(a, b, (((1,), (1,)), ((), ())), preferred_element_type=F32)


def iota(shape, dim):
    return lax.broadcasted_iota(jnp.int32, shape, dim)


def ones_where(cond):
    return jnp.where(cond, 1.0, 0.0).astype(BF)


def eye(n):
    return ones_where(iota((n, n), 0) == iota((n, n), 1))


def time_embed(timestep, width):
    half = width // 2
    freqs = jnp.exp(-math.log(10000.0) * jnp.arange(half, dtype=jnp.float32) / half)
    angle = timestep.astype(jnp.float32)[0] * freqs
    return jax.nn.silu(jnp.concatenate([jnp.cos(angle), jnp.sin(angle)])).astype(jnp.bfloat16)


class Sizes:
    def __init__(self, nf, nh, cols):
        self.nf, self.nh, self.cols = nf, nh, cols
        self.nc, self.nx = nf // 2, nh // 2
        self.cells = 2 * cols
        self.tok = 4 * nf
        self.nr = CA // nf // 8
        self.na = 6 if nh == 8 else nh
        self.ns = 2 * self.nr // self.na
        self.tr = 1024 // (2 * nh * self.nc)


def wide(frame):
    return jnp.concatenate([frame[0], frame[1]], axis=1)


def flat(slabs, width):
    value = slabs.astype(F32)
    return value.reshape(value.size // width, width).astype(BF)


def main_kernel(
    z, clip_in, w_time_in, w_down_in, w_embed_in, w_qkv_in, w_out_in, w_up_in, embed, cot_in,
    out_o, gc_o, ra_o, y_o, tap_o, w_aug_o,
    clip, w_time, w_down, w_embed, w_qkv, w_out, w_up, cot,
    out, grad_clip, ra_full, y_full, tap_full, w_aug,
    clip_l, clip_r, hidden, hg, hg_l, hg_r, acc,
    w_t, w_qkvp, w2, w2s, mh, mhl, wdu,
    p_send, g_send, p_got, g_got, p_all, g_all, dg_all, att_all,
    ls_send, ls_got, slab_send, slab_got,
    fp, fp_pair, fp_sum, fp_got, tp, tp_pair, tp_sum, tp_got, tq_sum, tq_got,
    y_send, y_got, x_buf,
    in_s, out_s,
    halo_s, halo_r, hgs, hgr, a2a_s, a2a_r, ag_s, ag_r, rs_s, rs_r, sl_s, sl_r,
    pair_s, pair_r, fr_s, fr_r, ff_s, ff_r, fw_s, fw_r,
    th_s, th_r, tf_s, tf_r, tg_s, tg_r, ta_s, ta_r, tw_s, tw_r,
    ys_s, ys_r, yh_s, yh_r, yf_s, yf_r, yw_s, yw_r,
):
    nf, nh, nc, nx = z.nf, z.nh, z.nc, z.nx
    f, h = lax.axis_index("frames"), lax.axis_index("heads")
    chip, core = f // 2, lax.rem(f, 2)
    partner = (chip * 2 + 1 - core, h)

    def send(src, dst, ssem, rsem, to):
        pltpu.make_async_remote_copy(
            src_ref=src, dst_ref=dst, send_sem=ssem, recv_sem=rsem, device_id=to, device_id_type=MESH
        ).start()

    def wait_send(src, sem):
        pltpu.make_async_remote_copy(
            src_ref=src, dst_ref=src, send_sem=sem, recv_sem=sem, device_id=(f, h), device_id_type=MESH
        ).wait_send()

    def wait_recv(dst, sem):
        pltpu.make_async_remote_copy(
            src_ref=dst, dst_ref=dst, send_sem=sem, recv_sem=sem, device_id=(f, h), device_id_type=MESH
        ).wait_recv()

    def other_f(k):
        return lax.rem(f + k, nf)

    def other_h(k):
        return lax.rem(h + k, nh)

    def other_c(k):
        return lax.rem(chip + k, nc)

    pulls = [
        (cot_in, cot), (clip_in, clip), (w_time_in, w_time), (w_embed_in, w_embed),
        (w_down_in, w_down), (w_qkv_in, w_qkv), (w_up_in, w_up), (w_out_in, w_out),
    ]
    pulls = [pltpu.make_async_copy(a, b, in_s.at[i]) for i, (a, b) in enumerate(pulls)]
    for pull in pulls:
        pull.start()

    def push(i, src, dst):
        pltpu.make_async_copy(src, dst, out_s.at[i]).start()

    barrier = pltpu.get_barrier_semaphore()
    for k in range(1, nf):
        pl.semaphore_signal(barrier, inc=1, device_id=(other_f(k), h), device_id_type=MESH)
    for k in range(1, nh):
        pl.semaphore_signal(barrier, inc=1, device_id=(f, other_h(k)), device_id_type=MESH)

    srow, scell = iota((8 * nf, z.cells), 0), iota((8 * nf, z.cells), 1)
    spos, sp = (srow // 8) * 4, lax.rem(srow, 8)
    column = lax.rem(scell, z.cols) // 2
    pool_p = ones_where((sp < 4) & (spos + sp == column))
    pool_g = ones_where((sp >= 4) & (spos + sp - 4 == column))
    pulls[0].wait()
    g_slab = mm_t1(pool_g, wide(cot[0])) + mm_t1(pool_g, wide(cot[1]))
    g_send[...] = jnp.zeros_like(g_send)
    g_send[:, :, 0:C] = g_slab.reshape(nf, 8, C).astype(BF)
    pulls[1].wait()

    pl.semaphore_wait(barrier, nf + nh - 2)

    @pl.when(f > 0)
    def _():
        send(clip.at[0], clip_r, halo_s.at[0], halo_r.at[0], (f - 1, h))

    @pl.when(f < nf - 1)
    def _():
        send(clip.at[1], clip_l, halo_s.at[1], halo_r.at[1], (f + 1, h))

    for k in range(1, nf):
        to = other_f(k)
        send(g_send.at[to], g_got.at[f], a2a_s.at[0, to], a2a_r.at[0, f], (to, h))
    g_got[f] = g_send[f]

    pulls[2].wait()
    unit = eye(C)
    for k in range(3):
        w_t[k] = mm_t0(w_time[k], unit).astype(BF)
    first, last = wide(clip[0]), wide(clip[1])
    acc[0] = mm(w_t[1], first) + mm(w_t[2], last)
    acc[1] = mm(w_t[0], first) + mm(w_t[1], last)

    sel_rows, sel_cols = iota((z.tok, 8 * nf), 0), iota((z.tok, 8 * nf), 1)
    want = (sel_rows // 4) * 8 + lax.rem(sel_rows, 4)
    sel_p = ones_where(sel_cols == want)
    sel_g = ones_where(sel_cols == want + 4)

    for k in range(1, nf):
        fr = other_f(k)
        wait_recv(g_got.at[fr], a2a_r.at[0, fr])
    g_all[h] = mm(sel_g, flat(g_got[...], CA)).astype(BF)
    for k in range(1, nh):
        to = other_h(k)
        send(g_all.at[h], g_all.at[h], ag_s.at[0, to], ag_r.at[0, h], (f, to))

    @pl.when(f > 0)
    def _():
        wait_recv(clip_l, halo_r.at[1])

    @pl.when(f == 0)
    def _():
        clip_l[...] = jnp.zeros_like(clip_l)

    @pl.when(f < nf - 1)
    def _():
        wait_recv(clip_r, halo_r.at[0])

    @pl.when(f == nf - 1)
    def _():
        clip_r[...] = jnp.zeros_like(clip_r)

    hidden[0] = (first.astype(F32) + acc[0] + mm(w_t[0], wide(clip_l))).astype(BF)
    hidden[1] = (last.astype(F32) + acc[1] + mm(w_t[2], wide(clip_r))).astype(BF)
    p_slab = (mm_t1(pool_p, hidden[0]) + mm_t1(pool_p, hidden[1])) * 0.125
    lane, prow = iota((nf, 8, CA), 2), iota((nf, 8, CA), 1)
    p_send[...] = ones_where((lane == C) & (prow < 4))
    p_send[:, :, 0:C] = p_slab.reshape(nf, 8, C).astype(BF)
    for k in range(1, nf):
        to = other_f(k)
        send(p_send.at[to], p_got.at[f], a2a_s.at[1, to], a2a_r.at[1, f], (to, h))
    p_got[f] = p_send[f]

    for pull in pulls[3:]:
        pull.wait()
    shift = mm(embed[...], w_embed[...])
    w_aug[0:C] = w_down[...]
    w_aug[C:CA] = jnp.where(iota((CA - C, CC), 0) == 0, jnp.broadcast_to(shift[0:1], (CA - C, CC)), 0.0).astype(BF)
    push(0, w_aug, w_aug_o)
    w_qkvp[...] = jnp.zeros_like(w_qkvp)
    for i in range(6):
        w_qkvp[128 * i : 128 * i + HD] = w_qkv[HD * i : HD * i + HD]
    w2_value = mm_t1(w_aug[...], w_qkvp[...]).astype(BF)
    w2[...] = w2_value
    w2s[0:C] = jnp.zeros((C, 768), BF)
    w2s[C:LW] = w2_value[0:C]
    mix = mm_t1(w_out[...], w_up[...]).astype(BF)
    for ref in (mh, mhl):
        ref[...] = jnp.zeros_like(ref)
        ref[0:HD, 0:C] = mix[0:HD]
        ref[128 : 128 + HD, 0:C] = mix[HD : 2 * HD]
    wdu[...] = jnp.zeros_like(wdu)
    wdu[:, 0:C] = mm_t1(w_aug[...], w_up[...]).astype(BF)

    for k in range(1, nf):
        fr = other_f(k)
        wait_recv(p_got.at[fr], a2a_r.at[1, fr])
    p_all[h] = mm(sel_p, flat(p_got[...], CA)).astype(BF)
    for k in range(1, nh):
        to = other_h(k)
        send(p_all.at[h], p_all.at[h], ag_s.at[1, to], ag_r.at[1, h], (f, to))

    bt = 2 * z.tok
    arow, acol = iota((bt, bt), 0), iota((bt, bt), 1)
    mask = (arow // z.tok == acol // z.tok) & (lax.rem(arow, 4) == lax.rem(acol, 4))

    def rows_needed(off):
        mine = 2 * (h // 2) + 1 - lax.rem(h, 2)
        base = 2 * lax.rem(h // 2 + off, nx)
        return [mine] if off == 0 else [base, base + 1]

    def block(off):
        b = lax.rem(h // 2 + off, nx)
        two = pl.ds(2 * b, 2)
        rows = pl.ds(pl.multiple_of(b * bt, bt), bt)
        pb = p_all[two].reshape(bt, CA)
        gb = g_all[two].reshape(bt, CA)
        qkv = mm(pb, w2[...]).astype(BF)
        ag = mm_t1(gb, mh[...]).astype(BF)
        grads, atts = [], []
        for n in range(2):
            q, k, v = (qkv[:, (3 * n + i) * 128 : (3 * n + i + 1) * 128] for i in range(3))
            a = ag[:, n * 128 : (n + 1) * 128]
            scores = jnp.where(mask, mm_t1(q, k) * SCALE, -1e30)
            e = jnp.exp(scores - jnp.max(scores, axis=1, keepdims=True))
            probs = e / jnp.sum(e, axis=1, keepdims=True)
            weights = probs.astype(BF)
            atts.append(mm(weights, v).astype(BF))
            wg = mm_t1(a, v)
            sg = (probs * (wg - jnp.sum(probs * wg, axis=1, keepdims=True)) * SCALE).astype(BF)
            grads += [mm(sg, k).astype(BF), mm_t0(sg, q).astype(BF), mm_t0(weights, a).astype(BF)]
        dg = jnp.concatenate(grads, axis=1)
        att = jnp.concatenate(atts, axis=1)
        dg_all[rows] = dg
        att_all[rows] = att
        ls_send[two] = (mm(att, mhl[...]) + mm_t1(dg, w2s[...])).astype(BF).reshape(2, z.tok, LW)

    offs = [0, 1, 3, 2] if nx == 4 else list(range(nx))
    for pair in [offs[i : i + 2] for i in range(0, nx, 2)]:
        for off in pair:
            for fr in rows_needed(off):
                wait_recv(g_all.at[fr], ag_r.at[0, fr])
                wait_recv(p_all.at[fr], ag_r.at[1, fr])
        for off in pair:
            block(off)
        for off in pair:
            for to in rows_needed(off):
                send(ls_send.at[to], ls_got.at[h], rs_s.at[to], rs_r.at[h], (f, to))

    tokens = nh * z.tok
    p_mat, g_mat = p_all[...].reshape(tokens, CA), g_all[...].reshape(tokens, CA)
    r_pad = mm_t0(p_mat, dg_all[...]).astype(BF)
    a_pad = mm_t0(g_mat, att_all[...]).astype(BF)
    rrow, rcol = iota((768, RAW), 0), iota((768, RAW), 1)
    sel_r = ones_where((rrow // 128 == rcol // HD) & (lax.rem(rrow, 128) == lax.rem(rcol, HD)))
    arow2, acol2 = iota((256, RAW), 0), iota((256, RAW), 1)
    sel_a = ones_where((arow2 // 128 + 6 == acol2 // HD) & (lax.rem(arow2, 128) == lax.rem(acol2, HD)))
    ra = mm(r_pad, sel_r) + mm(a_pad, sel_a)
    slabs = (nc, 2, z.nr, 8)
    fp[:, :, :, :, 0:RAW] = ra.reshape(*slabs, RAW).astype(BF)
    fp[:, :, :, :, RAW : RAW + CA] = mm_t0(p_mat, g_mat).reshape(*slabs, CA).astype(BF)
    fp[:, :, :, :, RAW + CA : FPW] = mm_t0(g_mat, p_mat).reshape(*slabs, CA).astype(BF)
    send(fp.at[:, 1 - core], fp_pair, pair_s.at[0], pair_r.at[0], partner)

    local = mm(flat(p_send[...], CA), wdu[...]) + mm_t1(flat(g_send[...], CA), wdu[...])

    wait_recv(fp_pair, pair_r.at[0])
    fp_sum[...] = (fp[:, core].astype(F32) + fp_pair[...].astype(F32)).astype(BF)
    for k in range(1, nc):
        to = other_c(k)
        send(fp_sum.at[to], fp_got.at[chip], fr_s.at[to], fr_r.at[chip], (to * 2 + core, h))

    ls = ls_send[h].astype(F32)
    for k in range(1, nh):
        fr = other_h(k)
        wait_recv(ls_got.at[fr], rs_r.at[fr])
        ls = ls + ls_got[fr].astype(F32)
    erow, ecol = iota((8 * nf, z.tok), 0), iota((8 * nf, z.tok), 1)
    ep, et = lax.rem(erow, 8), (erow // 8) * 4
    put_l = ones_where((ep < 4) & (et + ep == ecol))
    put_s = ones_where((ep >= 4) & (et + ep - 4 == ecol))
    slab = mm(put_l, ls[:, 0:C].astype(BF)) + mm(put_s, ls[:, C:LW].astype(BF))
    slab_send[:, :, 0:C] = slab.reshape(nf, 8, C).astype(BF)
    slab_send[:, :, C:CA] = jnp.zeros((nf, 8, CA - C), BF)
    for k in range(1, nf):
        to = other_f(k)
        send(slab_send.at[to], slab_got.at[f], sl_s.at[to], sl_r.at[f], (to, h))
    slab_got[f] = slab_send[f]

    fsum = fp_sum[chip].astype(F32)
    for k in range(1, nc):
        fr = other_c(k)
        wait_recv(fp_got.at[fr], fr_r.at[fr])
        fsum = fsum + fp_got[fr].astype(F32)
    fsum = fsum.reshape(8 * z.nr, FPW).astype(BF)
    down = mm(fsum[:, 0:480], w_qkv[...])
    lift = mm(fsum[:, 480:RAW], w_out[...])
    part = jnp.concatenate([down, lift], axis=0)
    y_send[...] = part.reshape(z.na, z.ns, 8, CC).astype(BF)
    for j in range(z.na):

        @pl.when(h != j)
        def _():
            send(y_send.at[j], y_got.at[h], ys_s.at[j], ys_r.at[h], (f, j))

    x_part = jnp.concatenate(
        [mm(fsum[:, RAW : RAW + C], w_up[...]), mm(fsum[:, RAW + CA : FPW], w_aug[...])], axis=0
    )
    x_buf[...] = x_part.reshape(z.na, z.ns, 8, CC)
    ra_full[chip, core] = fsum[:, 0:RAW].astype(F32).reshape(z.nr, 8, RAW).astype(BF)
    for k in range(1, nc):
        to = other_c(k)
        send(ra_full.at[chip, core], ra_full.at[chip, core], ff_s.at[to], ff_r.at[chip], (to * 2 + core, h))
    send(ra_full.at[chip, core], ra_full.at[chip, core], fw_s.at[chip], fw_r.at[chip], partner)

    for k in range(1, nf):
        fr = other_f(k)
        wait_recv(slab_got.at[fr], sl_r.at[fr])
    lsf = (slab_got[...].astype(F32).reshape(8 * nf, CA) + local).astype(BF)[:, 0:C]
    spread = mm_t0(lsf, pool_g) * 0.125
    grads_now = []
    for t in range(2):
        value = (wide(cot[t]).astype(F32) + spread).astype(BF)
        grads_now.append(value)
        for r in range(2):
            hg[t, r] = value[:, r * z.cols : (r + 1) * z.cols]

    @pl.when(f > 0)
    def _():
        send(hg.at[0], hg_r, hgs.at[0], hgr.at[0], (f - 1, h))

    @pl.when(f < nf - 1)
    def _():
        send(hg.at[1], hg_l, hgs.at[1], hgr.at[1], (f + 1, h))

    hg0, hg1 = grads_now
    left, right = wide(clip_l), wide(clip_r)
    taps = jnp.concatenate(
        [
            mm_t1(left, hg0) + mm_t1(first, hg1),
            mm_t1(first, hg0) + mm_t1(last, hg1),
            mm_t1(last, hg0) + mm_t1(right, hg1),
            jnp.zeros((64, C), F32),
        ],
        axis=0,
    )
    tp[...] = jnp.zeros_like(tp)
    tp[:, :, :, :, 0:C] = taps.reshape(2, nh, nc, z.tr, C).astype(BF)
    send(tp.at[1 - core], tp_pair, pair_s.at[1], pair_r.at[1], partner)

    lifted = mm_t0(lsf, pool_p)
    for t in range(2):
        value = (hidden[t].astype(F32) + lifted).astype(BF)
        for r in range(2):
            out[t, r] = value[:, r * z.cols : (r + 1) * z.cols]
    push(1, out, out_o)

    wait_recv(tp_pair, pair_r.at[1])
    tp_sum[...] = (tp[core].astype(F32) + tp_pair[...].astype(F32)).astype(BF)
    for k in range(1, nh):
        to = other_h(k)
        send(tp_sum.at[to], tp_got.at[h], th_s.at[to], th_r.at[h], (f, to))

    @pl.when(h < z.na)
    def _():
        value = y_send[h].astype(F32) + x_buf[h]
        for k in range(1, nh):
            fr = other_h(k)
            wait_recv(y_got.at[fr], ys_r.at[fr])
            value = value + y_got[fr].astype(F32)
        y_full[chip, core, h] = value.astype(BF)
        for k in range(1, nh):
            to = other_h(k)
            send(y_full.at[chip, core, h], y_full.at[chip, core, h], yh_s.at[to], yh_r.at[h], (f, to))

    for k in range(1, nc):
        fr = other_c(k)
        wait_recv(ra_full.at[fr, core], ff_r.at[fr])
        send(ra_full.at[fr, core], ra_full.at[fr, core], fw_s.at[fr], fw_r.at[fr], partner)

    value = tp_sum[h].astype(F32)
    for k in range(1, nh):
        fr = other_h(k)
        wait_recv(tp_got.at[fr], th_r.at[fr])
        value = value + tp_got[fr].astype(F32)
    tq_sum[...] = value.astype(BF)
    for k in range(1, nc):
        to = other_c(k)
        send(tq_sum.at[to], tq_got.at[chip], tf_s.at[to], tf_r.at[chip], (to * 2 + core, h))

    for j in range(z.na):

        @pl.when(h != j)
        def _():
            wait_recv(y_full.at[chip, core, j], yh_r.at[j])

    for k in range(1, nc):
        to = other_c(k)
        send(y_full.at[chip, core], y_full.at[chip, core], yf_s.at[to], yf_r.at[chip], (to * 2 + core, h))
    send(y_full.at[chip, core], y_full.at[chip, core], yw_s.at[chip], yw_r.at[chip], partner)

    @pl.when(f > 0)
    def _():
        wait_recv(hg_l, hgr.at[1])

    @pl.when(f == 0)
    def _():
        hg_l[...] = jnp.zeros_like(hg_l)

    @pl.when(f < nf - 1)
    def _():
        wait_recv(hg_r, hgr.at[0])

    @pl.when(f == nf - 1)
    def _():
        hg_r[...] = jnp.zeros_like(hg_r)

    acc[0] = hg0.astype(F32) + mm(w_time[0], hg1) + mm(w_time[1], hg0) + mm(w_time[2], wide(hg_l))
    acc[1] = hg1.astype(F32) + mm(w_time[0], wide(hg_r)) + mm(w_time[1], hg1) + mm(w_time[2], hg0)
    for t in range(2):
        for r in range(2):
            grad_clip[t, r] = acc[t, :, r * z.cols : (r + 1) * z.cols]
    push(2, grad_clip, gc_o)

    for k in range(nc):
        wait_recv(ra_full.at[other_c(k), 1 - core], fw_r.at[other_c(k)])
    push(3, ra_full, ra_o)

    value = tq_sum[chip].astype(F32)
    for k in range(1, nc):
        fr = other_c(k)
        wait_recv(tq_got.at[fr], tf_r.at[fr])
        value = value + tq_got[fr].astype(F32)
    tap_full[core, h, chip] = value.astype(BF)
    for k in range(1, nc):
        to = other_c(k)
        here = tap_full.at[core, h, chip]
        send(here, here, tg_s.at[to], tg_r.at[chip], (to * 2 + core, h))
    for k in range(1, nc):
        fr = other_c(k)
        wait_recv(tap_full.at[core, h, fr], tg_r.at[fr])
    for k in range(1, nh):
        to = other_h(k)
        send(tap_full.at[core, h], tap_full.at[core, h], ta_s.at[to], ta_r.at[h], (f, to))
    send(tap_full.at[core, h], tap_full.at[core, h], tw_s.at[h], tw_r.at[h], partner)

    for k in range(1, nc):
        fr = other_c(k)
        wait_recv(y_full.at[fr, core], yf_r.at[fr])
        send(y_full.at[fr, core], y_full.at[fr, core], yw_s.at[fr], yw_r.at[fr], partner)
    for k in range(1, nh):
        fr = other_h(k)
        wait_recv(tap_full.at[core, fr], ta_r.at[fr])
        send(tap_full.at[core, fr], tap_full.at[core, fr], tw_s.at[fr], tw_r.at[fr], partner)
    for k in range(nc):
        wait_recv(y_full.at[other_c(k), 1 - core], yw_r.at[other_c(k)])
    push(4, y_full, y_o)
    for k in range(nh):
        wait_recv(tap_full.at[1 - core, other_h(k)], tw_r.at[other_h(k)])
    push(5, tap_full, tap_o)

    @pl.when(f > 0)
    def _():
        wait_send(clip.at[0], halo_s.at[0])
        wait_send(hg.at[0], hgs.at[0])

    @pl.when(f < nf - 1)
    def _():
        wait_send(clip.at[1], halo_s.at[1])
        wait_send(hg.at[1], hgs.at[1])

    for k in range(1, nf):
        to = other_f(k)
        wait_send(g_send.at[to], a2a_s.at[0, to])
        wait_send(p_send.at[to], a2a_s.at[1, to])
        wait_send(slab_send.at[to], sl_s.at[to])
    for k in range(1, nh):
        to = other_h(k)
        wait_send(g_all.at[h], ag_s.at[0, to])
        wait_send(p_all.at[h], ag_s.at[1, to])
        wait_send(ls_send.at[to], rs_s.at[to])
        wait_send(tp_sum.at[to], th_s.at[to])
        wait_send(tap_full.at[core, h], ta_s.at[to])
    for k in range(nh):
        wait_send(tap_full.at[core, other_h(k)], tw_s.at[other_h(k)])
    wait_send(fp_pair, pair_s.at[0])
    wait_send(tp_pair, pair_s.at[1])
    for k in range(1, nc):
        to = other_c(k)
        wait_send(fp_sum.at[to], fr_s.at[to])
        wait_send(ra_full.at[chip, core], ff_s.at[to])
        wait_send(tq_sum.at[to], tf_s.at[to])
        wait_send(tap_full.at[core, h, chip], tg_s.at[to])
        wait_send(y_full.at[chip, core], yf_s.at[to])
    for k in range(nc):
        to = other_c(k)
        wait_send(ra_full.at[to, core], fw_s.at[to])
        wait_send(y_full.at[to, core], yw_s.at[to])
    for j in range(z.na):

        @pl.when(h != j)
        def _():
            wait_send(y_send.at[j], ys_s.at[j])

    @pl.when(h < z.na)
    def _():
        for k in range(1, nh):
            wait_send(y_full.at[chip, core, h], yh_s.at[other_h(k)])

    pushes = [(w_aug, w_aug_o), (out, out_o), (grad_clip, gc_o), (ra_full, ra_o), (y_full, y_o), (tap_full, tap_o)]
    for i, (a, b) in enumerate(pushes):
        pltpu.make_async_copy(a, b, out_s.at[i]).wait()


def final_kernel(
    z, ra_in, y_in, tap_in, w_aug_in, w_up_in, embed_col, out_in, gc_in,
    out_o, gc_o, time_o, down_o, embed_o, qkv_o, wout_o, up_o,
    ra, y, tap, w_aug, w_up, out, gc, time, down, emb, qkv, wout, up, in_s, out_s,
):
    pulls = [(out_in, out), (gc_in, gc), (ra_in, ra), (w_aug_in, w_aug), (w_up_in, w_up), (y_in, y), (tap_in, tap)]
    pulls = [pltpu.make_async_copy(a, b, in_s.at[i]) for i, (a, b) in enumerate(pulls)]
    for pull in pulls:
        pull.start()
    pushes = []

    def push(src, dst):
        copy = pltpu.make_async_copy(src, dst, out_s.at[len(pushes)])
        copy.start()
        pushes.append(copy)

    pulls[0].wait()
    push(out, out_o)
    pulls[1].wait()
    push(gc, gc_o)
    pulls[2].wait()
    pulls[3].wait()
    sums = flat(ra[...], RAW)
    qkv[...] = mm_t0(sums[:, 0:480], w_aug[...])
    push(qkv, qkv_o)
    pulls[4].wait()
    wout[...] = mm_t0(sums[0:C, 480:RAW], w_up[...])
    push(wout, wout_o)
    pulls[5].wait()
    both = y[...].astype(F32)
    grad_down = both[:, 0].reshape(CA, CC)
    down[...] = grad_down[0:C]
    push(down, down_o)
    emb[...] = embed_col[...] * grad_down[C : C + 1]
    push(emb, embed_o)
    up[...] = both[:, 1].reshape(CA, CC)[0:C]
    push(up, up_o)
    pulls[6].wait()
    time[...] = tap[...].astype(F32).reshape(1024, CA)[0:960, 0:C]
    push(time, time_o)
    for copy in pushes:
        copy.wait()


def shards(z, clip, w_time, w_down, w_embed, w_qkv, w_out, w_up, timestep, cotangent):
    nf, nh, nc = z.nf, z.nh, z.nc
    embed = time_embed(timestep, w_embed.shape[0])
    embed_rows = jnp.broadcast_to(embed[None, :], (16, C))
    vm = pl.BlockSpec(memory_space=pltpu.VMEM)
    hbm = pl.BlockSpec(memory_space=pl.ANY)
    dma = pltpu.SemaphoreType.DMA

    def bf(*shape):
        return pltpu.VMEM(shape, BF)

    def f32(*shape):
        return pltpu.VMEM(shape, F32)

    def like(kind, dtype):
        return jax.ShapeDtypeStruct(kind, dtype)

    frames = (2, 2, C, z.cols)
    ra_shape, y_shape = (nc, 2, z.nr, 8, RAW), (nc, 2, z.na, z.ns, 8, CC)
    tap_shape = (2, nh, nc, z.tr, CA)
    w_up_t = w_up.T
    outs = pl.pallas_call(
        functools.partial(main_kernel, z),
        out_shape=(
            like(frames, BF), like(frames, F32), like(ra_shape, BF), like(y_shape, BF),
            like(tap_shape, BF), like((CA, CC), BF),
        ),
        in_specs=[hbm] * 7 + [vm, hbm],
        out_specs=(hbm,) * 6,
        scratch_shapes=[
            bf(*frames), bf(3, C, C), bf(C, CC), bf(C, CC), bf(480, CC), bf(2 * HD, CC), bf(C, CC), bf(*frames),
            bf(*frames), f32(*frames), bf(*ra_shape), bf(*y_shape), bf(*tap_shape), bf(CA, CC),
            bf(*frames[1:]), bf(*frames[1:]), bf(2, C, z.cells), bf(*frames), bf(*frames[1:]), bf(*frames[1:]),
            f32(2, C, z.cells),
            bf(3, C, C), bf(768, CC), bf(CA, 768), bf(LW, 768), bf(256, CA), bf(256, LW), bf(CA, CA),
            bf(nf, 8, CA), bf(nf, 8, CA), bf(nf, 8, CA), bf(nf, 8, CA),
            bf(nh, z.tok, CA), bf(nh, z.tok, CA), bf(nh * z.tok, 768), bf(nh * z.tok, 256),
            bf(nh, z.tok, LW), bf(nh, z.tok, LW), bf(nf, 8, CA), bf(nf, 8, CA),
            bf(nc, 2, z.nr, 8, FPW), bf(nc, z.nr, 8, FPW), bf(nc, z.nr, 8, FPW), bf(nc, z.nr, 8, FPW),
            bf(*tap_shape), bf(nh, nc, z.tr, CA), bf(nh, nc, z.tr, CA), bf(nh, nc, z.tr, CA),
            bf(nc, z.tr, CA), bf(nc, z.tr, CA),
            bf(z.na, z.ns, 8, CC), bf(nh, z.ns, 8, CC), f32(z.na, z.ns, 8, CC),
            dma((8,)), dma((6,)),
            dma((2,)), dma((2,)), dma((2,)), dma((2,)),
            dma((2, nf)), dma((2, nf)), dma((2, nh)), dma((2, nh)),
            dma((nh,)), dma((nh,)), dma((nf,)), dma((nf,)),
            dma((2,)), dma((2,)), dma((nc,)), dma((nc,)), dma((nc,)), dma((nc,)), dma((nc,)), dma((nc,)),
            dma((nh,)), dma((nh,)), dma((nc,)), dma((nc,)), dma((nc,)), dma((nc,)),
            dma((nh,)), dma((nh,)), dma((nh,)), dma((nh,)),
            dma((nh,)), dma((nh,)), dma((nh,)), dma((nh,)), dma((nc,)), dma((nc,)), dma((nc,)), dma((nc,)),
        ],
        compiler_params=pltpu.CompilerParams(
            collective_id=0, has_side_effects=True, vmem_limit_bytes=60 * 1024 * 1024
        ),
    )(
        jnp.swapaxes(clip, 2, 3), w_time, w_down, w_embed, w_qkv.T, w_out, w_up_t, embed_rows,
        jnp.swapaxes(cotangent, 2, 3),
    )
    out, grad_clip, ra_full, y_full, tap_full, w_aug = outs
    grads = pl.pallas_call(
        functools.partial(final_kernel, z),
        out_shape=(
            like(frames, BF), like(frames, F32), like((960, C), F32), like((C, CC), F32), like((C, CC), F32),
            like((480, CC), F32), like((2 * HD, CC), F32), like((C, CC), F32),
        ),
        in_specs=[hbm] * 5 + [vm, hbm, hbm],
        out_specs=(hbm,) * 8,
        scratch_shapes=[
            bf(*ra_shape), bf(nf, 2, z.nr, 8, CC), bf(*tap_shape), bf(CA, CC), bf(C, CC), bf(*frames), f32(*frames),
            f32(960, C), f32(C, CC), f32(C, CC), f32(480, CC), f32(2 * HD, CC), f32(C, CC),
            dma((7,)), dma((8,)),
        ],
        compiler_params=pltpu.CompilerParams(vmem_limit_bytes=60 * 1024 * 1024),
    )(
        ra_full, y_full.reshape(nf, 2, z.nr, 8, CC), tap_full, w_aug, w_up_t, embed.astype(F32)[:, None],
        out, grad_clip,
    )
    out, grad_clip, grad_time, grad_down, grad_embed, grad_qkv, grad_out, grad_up = grads
    return (
        jnp.swapaxes(out, 2, 3),
        jnp.swapaxes(grad_clip, 2, 3),
        grad_time.reshape(3, C, C),
        grad_down,
        grad_embed,
        grad_qkv.T,
        grad_out,
        grad_up.T,
    )


def solution(mesh, cols=128):
    z = Sizes(mesh.shape["frames"], mesh.shape["heads"], cols)
    return jax.shard_map(
        functools.partial(shards, z),
        mesh=mesh,
        in_specs=(
            P("frames", "heads", None, None),
            P(),
            P(),
            P(),
            P(None, "heads"),
            P("heads", None),
            P(),
            P(),
            P("frames", "heads", None, None),
        ),
        out_specs=(
            P("frames", "heads", None, None),
            P("frames", "heads", None, None),
            P(),
            P(),
            P(),
            P(None, "heads"),
            P("heads", None),
            P(),
        ),
        check_vma=False,
    )
```

time: 130 us -> 106 us (0.82)
  local copies, waits for them, and re-layouts: 19.9 us -> 1.44 us
  Pallas kernels: 108 us -> 102 us
    unnamed x20 -> x0, local copies, waits for them, and re-layouts: 19.1 us -> none
    pallas_call x2, Pallas kernels: 108 us -> 102 us  [the longest x1 95 us: shards(): pl.pallas_call(functools.partial(main_kernel, z), out_shape=(like(frames,...]
where the time goes in v1:
time: 106 us; the launch traced here: 105 us
  Pallas kernels  102 us (96%)
  between operations  1.45 us (1%)
  local copies, waits for them, and re-layouts  1.44 us (1%)
    pallas_call x1, Pallas kernels, shards(): pl.pallas_call(functools.partial(main_kernel, z), out_shape=(like(frames,...  95 us
    pallas_call x1, Pallas kernels, shards(): pl.pallas_call(functools.partial(final_kernel, z), out_shape=(like(frames...  7.38 us

profile of v1, /device:TPU:1, one launch (start us, length us, event | category | flops | bytes accessed | tf_op | source)
XLA Modules:
  0.0 105.5 jit_solution(15608865347305133702)
XLA Ops:
  1.3 0.1 fusion
  1.4 0.1 convert_convert_fusion
  1.5 0.6 broadcast_in_dim.2.embed
  2.1 0.8 copy.22.embed_col
  2.9 95.0 %shard_map.152 = (bf16[2,2,320,128]{3,2,1,0:T(8,128)(2,1)}, f32[2,2,320,128]{3,2,1,0:T(8,128)}, bf16[8,2,3,8,640]{4,3,2,1,0:T(8,128)(2,1)}, bf16[8,2,6,1,8,1280]...) custom-call(bf16[2,2,320,128]{3,2,1,0:T(8,128)(2,1)} %bitcast.17, ...), custom_call_target="tpu_custom_call" | custom-call | tf_op jit(solution)/shard_map/pallas_call | solution.py:619
  97.9 7.4 %shard_map.153 = (bf16[2,2,320,128]{3,2,1,0:T(8,128)(2,1)}, f32[2,2,320,128]{3,2,1,0:T(8,128)}, f32[960,320]{1,0:T(8,128)}, f32[320,1280]{1,0:T(8,128)}, f32[320...) custom-call(bf16[8,2,3,8,640]{4,3,2,1,0:T(8,128)(2,1)} %get-tuple-element.22.ra_in, ...), custom_call_target="tpu_custom_call" | custom-call | tf_op jit(solution)/shard_map/pallas_call | solution.py:657
  (1 shorter events, 0.0 us)

commit v2 on v1

--- a/solution.py
+++ b/solution.py
@@ -18,7 +18,6 @@
 CC = 1280
 LW = 2 * C
 RAW = 8 * HD
-FPW = RAW + 2 * CA
 
 
 def mm(a, b):
@@ -83,8 +82,8 @@
     p_send, g_send, p_got, g_got, p_all, g_all, dg_all, att_all,
     ls_send, ls_got, slab_send, slab_got,
     fp, fp_pair, fp_sum, fp_got, tp, tp_pair, tp_sum, tp_got, tq_sum, tq_got,
-    y_send, y_got, x_buf,
-    in_s, out_s,
+    y_send, y_got, x_buf, x_all, xs, xs_pair, xs_sum, xs_got,
+    in_s, out_s, fx_s, fx_r,
     halo_s, halo_r, hgs, hgr, a2a_s, a2a_r, ag_s, ag_r, rs_s, rs_r, sl_s, sl_r,
     pair_s, pair_r, fr_s, fr_r, ff_s, ff_r, fw_s, fw_r,
     th_s, th_r, tf_s, tf_r, tg_s, tg_r, ta_s, ta_r, tw_s, tw_r,
@@ -170,49 +169,9 @@
     acc[0] = mm(w_t[1], first) + mm(w_t[2], last)
     acc[1] = mm(w_t[0], first) + mm(w_t[1], last)
 
-    sel_rows, sel_cols = iota((z.tok, 8 * nf), 0), iota((z.tok, 8 * nf), 1)
-    want = (sel_rows // 4) * 8 + lax.rem(sel_rows, 4)
-    sel_p = ones_where(sel_cols == want)
-    sel_g = ones_where(sel_cols == want + 4)
-
-    for k in range(1, nf):
-        fr = other_f(k)
-        wait_recv(g_got.at[fr], a2a_r.at[0, fr])
-    g_all[h] = mm(sel_g, flat(g_got[...], CA)).astype(BF)
-    for k in range(1, nh):
-        to = other_h(k)
-        send(g_all.at[h], g_all.at[h], ag_s.at[0, to], ag_r.at[0, h], (f, to))
-
-    @pl.when(f > 0)
-    def _():
-        wait_recv(clip_l, halo_r.at[1])
-
-    @pl.when(f == 0)
-    def _():
-        clip_l[...] = jnp.zeros_like(clip_l)
-
-    @pl.when(f < nf - 1)
-    def _():
-        wait_recv(clip_r, halo_r.at[0])
-
-    @pl.when(f == nf - 1)
-    def _():
-        clip_r[...] = jnp.zeros_like(clip_r)
-
-    hidden[0] = (first.astype(F32) + acc[0] + mm(w_t[0], wide(clip_l))).astype(BF)
-    hidden[1] = (last.astype(F32) + acc[1] + mm(w_t[2], wide(clip_r))).astype(BF)
-    p_slab = (mm_t1(pool_p, hidden[0]) + mm_t1(pool_p, hidden[1])) * 0.125
-    lane, prow = iota((nf, 8, CA), 2), iota((nf, 8, CA), 1)
-    p_send[...] = ones_where((lane == C) & (prow < 4))
-    p_send[:, :, 0:C] = p_slab.reshape(nf, 8, C).astype(BF)
-    for k in range(1, nf):
-        to = other_f(k)
-        send(p_send.at[to], p_got.at[f], a2a_s.at[1, to], a2a_r.at[1, f], (to, h))
-    p_got[f] = p_send[f]
-
     for pull in pulls[3:]:
         pull.wait()
-    shift = mm(embed[...], w_embed[...])
+    shift = mm(jnp.broadcast_to(embed[...], (16, C)), w_embed[...])
     w_aug[0:C] = w_down[...]
     w_aug[C:CA] = jnp.where(iota((CA - C, CC), 0) == 0, jnp.broadcast_to(shift[0:1], (CA - C, CC)), 0.0).astype(BF)
     push(0, w_aug, w_aug_o)
@@ -230,6 +189,46 @@
         ref[128 : 128 + HD, 0:C] = mix[HD : 2 * HD]
     wdu[...] = jnp.zeros_like(wdu)
     wdu[:, 0:C] = mm_t1(w_aug[...], w_up[...]).astype(BF)
+
+    sel_rows, sel_cols = iota((z.tok, 8 * nf), 0), iota((z.tok, 8 * nf), 1)
+    want = (sel_rows // 4) * 8 + lax.rem(sel_rows, 4)
+    sel_p = ones_where(sel_cols == want)
+    sel_g = ones_where(sel_cols == want + 4)
+
+    @pl.when(f > 0)
+    def _():
+        wait_recv(clip_l, halo_r.at[1])
+
+    @pl.when(f == 0)
+    def _():
+        clip_l[...] = jnp.zeros_like(clip_l)
+
+    @pl.when(f < nf - 1)
+    def _():
+        wait_recv(clip_r, halo_r.at[0])
+
+    @pl.when(f == nf - 1)
+    def _():
+        clip_r[...] = jnp.zeros_like(clip_r)
+
+    hidden[0] = (first.astype(F32) + acc[0] + mm(w_t[0], wide(clip_l))).astype(BF)
+    hidden[1] = (last.astype(F32) + acc[1] + mm(w_t[2], wide(clip_r))).astype(BF)
+    p_slab = (mm_t1(pool_p, hidden[0]) + mm_t1(pool_p, hidden[1])) * 0.125
+    lane, prow = iota((nf, 8, CA), 2), iota((nf, 8, CA), 1)
+    p_send[...] = ones_where((lane == C) & (prow < 4))
+    p_send[:, :, 0:C] = p_slab.reshape(nf, 8, C).astype(BF)
+    for k in range(1, nf):
+        to = other_f(k)
+        send(p_send.at[to], p_got.at[f], a2a_s.at[1, to], a2a_r.at[1, f], (to, h))
+    p_got[f] = p_send[f]
+
+    for k in range(1, nf):
+        fr = other_f(k)
+        wait_recv(g_got.at[fr], a2a_r.at[0, fr])
+    g_all[h] = mm(sel_g, flat(g_got[...], CA)).astype(BF)
+    for k in range(1, nh):
+        to = other_h(k)
+        send(g_all.at[h], g_all.at[h], ag_s.at[0, to], ag_r.at[0, h], (f, to))
 
     for k in range(1, nf):
         fr = other_f(k)
@@ -296,10 +295,20 @@
     sel_a = ones_where((arow2 // 128 + 6 == acol2 // HD) & (lax.rem(arow2, 128) == lax.rem(acol2, HD)))
     ra = mm(r_pad, sel_r) + mm(a_pad, sel_a)
     slabs = (nc, 2, z.nr, 8)
-    fp[:, :, :, :, 0:RAW] = ra.reshape(*slabs, RAW).astype(BF)
-    fp[:, :, :, :, RAW : RAW + CA] = mm_t0(p_mat, g_mat).reshape(*slabs, CA).astype(BF)
-    fp[:, :, :, :, RAW + CA : FPW] = mm_t0(g_mat, p_mat).reshape(*slabs, CA).astype(BF)
+    fp[...] = ra.reshape(*slabs, RAW).astype(BF)
     send(fp.at[:, 1 - core], fp_pair, pair_s.at[0], pair_r.at[0], partner)
+
+    @pl.when(h < z.na // 2)
+    def _():
+        x_all[...] = mm_t0(p_mat, g_mat).reshape(*slabs, CA).astype(BF)
+
+    @pl.when(h >= z.na // 2)
+    def _():
+        x_all[...] = mm_t0(g_mat, p_mat).reshape(*slabs, CA).astype(BF)
+
+    mine = pl.ds(lax.rem(h, z.na // 2) * z.ns, z.ns)
+    xs[...] = x_all[:, :, mine]
+    send(xs.at[:, 1 - core], xs_pair, pair_s.at[2], pair_r.at[2], partner)
 
     local = mm(flat(p_send[...], CA), wdu[...]) + mm_t1(flat(g_send[...], CA), wdu[...])
 
@@ -308,6 +317,11 @@
     for k in range(1, nc):
         to = other_c(k)
         send(fp_sum.at[to], fp_got.at[chip], fr_s.at[to], fr_r.at[chip], (to * 2 + core, h))
+    wait_recv(xs_pair, pair_r.at[2])
+    xs_sum[...] = (xs[:, core].astype(F32) + xs_pair[...].astype(F32)).astype(BF)
+    for k in range(1, nc):
+        to = other_c(k)
+        send(xs_sum.at[to], xs_got.at[chip], fx_s.at[to], fx_r.at[chip], (to * 2 + core, h))
 
     ls = ls_send[h].astype(F32)
     for k in range(1, nh):
@@ -331,7 +345,7 @@
         fr = other_c(k)
         wait_recv(fp_got.at[fr], fr_r.at[fr])
         fsum = fsum + fp_got[fr].astype(F32)
-    fsum = fsum.reshape(8 * z.nr, FPW).astype(BF)
+    fsum = fsum.reshape(8 * z.nr, RAW).astype(BF)
     down = mm(fsum[:, 0:480], w_qkv[...])
     lift = mm(fsum[:, 480:RAW], w_out[...])
     part = jnp.concatenate([down, lift], axis=0)
@@ -342,16 +356,7 @@
         def _():
             send(y_send.at[j], y_got.at[h], ys_s.at[j], ys_r.at[h], (f, j))
 
-    x_part = jnp.concatenate(
-        [mm(fsum[:, RAW : RAW + C], w_up[...]), mm(fsum[:, RAW + CA : FPW], w_aug[...])], axis=0
-    )
-    x_buf[...] = x_part.reshape(z.na, z.ns, 8, CC)
     ra_full[chip, core] = fsum[:, 0:RAW].astype(F32).reshape(z.nr, 8, RAW).astype(BF)
-    for k in range(1, nc):
-        to = other_c(k)
-        send(ra_full.at[chip, core], ra_full.at[chip, core], ff_s.at[to], ff_r.at[chip], (to * 2 + core, h))
-    send(ra_full.at[chip, core], ra_full.at[chip, core], fw_s.at[chip], fw_r.at[chip], partner)
-
     for k in range(1, nf):
         fr = other_f(k)
         wait_recv(slab_got.at[fr], sl_r.at[fr])
@@ -387,22 +392,24 @@
     tp[:, :, :, :, 0:C] = taps.reshape(2, nh, nc, z.tr, C).astype(BF)
     send(tp.at[1 - core], tp_pair, pair_s.at[1], pair_r.at[1], partner)
 
-    lifted = mm_t0(lsf, pool_p)
-    for t in range(2):
-        value = (hidden[t].astype(F32) + lifted).astype(BF)
-        for r in range(2):
-            out[t, r] = value[:, r * z.cols : (r + 1) * z.cols]
-    push(1, out, out_o)
-
-    wait_recv(tp_pair, pair_r.at[1])
-    tp_sum[...] = (tp[core].astype(F32) + tp_pair[...].astype(F32)).astype(BF)
-    for k in range(1, nh):
-        to = other_h(k)
-        send(tp_sum.at[to], tp_got.at[h], th_s.at[to], th_r.at[h], (f, to))
-
     @pl.when(h < z.na)
     def _():
-        value = y_send[h].astype(F32) + x_buf[h]
+        xsum = xs_sum[chip].astype(F32)
+        for k in range(1, nc):
+            fr = other_c(k)
+            wait_recv(xs_got.at[fr], fx_r.at[fr])
+            xsum = xsum + xs_got[fr].astype(F32)
+        x_mat = xsum.reshape(8 * z.ns, CA).astype(BF)
+
+        @pl.when(h < z.na // 2)
+        def _():
+            x_buf[...] = mm(x_mat[:, 0:C], w_up[...]).reshape(z.ns, 8, CC)
+
+        @pl.when(h >= z.na // 2)
+        def _():
+            x_buf[...] = mm(x_mat, w_aug[...]).reshape(z.ns, 8, CC)
+
+        value = y_send[h].astype(F32) + x_buf[...]
         for k in range(1, nh):
             fr = other_h(k)
             wait_recv(y_got.at[fr], ys_r.at[fr])
@@ -412,31 +419,24 @@
             to = other_h(k)
             send(y_full.at[chip, core, h], y_full.at[chip, core, h], yh_s.at[to], yh_r.at[h], (f, to))
 
-    for k in range(1, nc):
-        fr = other_c(k)
-        wait_recv(ra_full.at[fr, core], ff_r.at[fr])
-        send(ra_full.at[fr, core], ra_full.at[fr, core], fw_s.at[fr], fw_r.at[fr], partner)
-
-    value = tp_sum[h].astype(F32)
-    for k in range(1, nh):
-        fr = other_h(k)
-        wait_recv(tp_got.at[fr], th_r.at[fr])
-        value = value + tp_got[fr].astype(F32)
-    tq_sum[...] = value.astype(BF)
-    for k in range(1, nc):
-        to = other_c(k)
-        send(tq_sum.at[to], tq_got.at[chip], tf_s.at[to], tf_r.at[chip], (to * 2 + core, h))
-
-    for j in range(z.na):
-
-        @pl.when(h != j)
-        def _():
-            wait_recv(y_full.at[chip, core, j], yh_r.at[j])
-
-    for k in range(1, nc):
-        to = other_c(k)
-        send(y_full.at[chip, core], y_full.at[chip, core], yf_s.at[to], yf_r.at[chip], (to * 2 + core, h))
-    send(y_full.at[chip, core], y_full.at[chip, core], yw_s.at[chip], yw_r.at[chip], partner)
+    @pl.when(h >= z.na)
+    def _():
+        for k in range(1, nc):
+            fr = other_c(k)
+            wait_recv(xs_got.at[fr], fx_r.at[fr])
+
+    wait_recv(tp_pair, pair_r.at[1])
+    tp_sum[...] = (tp[core].astype(F32) + tp_pair[...].astype(F32)).astype(BF)
+    for k in range(1, nh):
+        to = other_h(k)
+        send(tp_sum.at[to], tp_got.at[h], th_s.at[to], th_r.at[h], (f, to))
+
+    lifted = mm_t0(lsf, pool_p)
+    for t in range(2):
+        value = (hidden[t].astype(F32) + lifted).astype(BF)
+        for r in range(2):
+            out[t, r] = value[:, r * z.cols : (r + 1) * z.cols]
+    push(1, out, out_o)
 
     @pl.when(f > 0)
     def _():
@@ -461,9 +461,32 @@
             grad_clip[t, r] = acc[t, :, r * z.cols : (r + 1) * z.cols]
     push(2, grad_clip, gc_o)
 
-    for k in range(nc):
-        wait_recv(ra_full.at[other_c(k), 1 - core], fw_r.at[other_c(k)])
-    push(3, ra_full, ra_o)
+    def y_half(i, c, k):
+        return y_full.at[c, k, pl.ds(i * (z.na // 2), z.na // 2)]
+
+    def y_start(i):
+        for j in range(i * (z.na // 2), (i + 1) * (z.na // 2)):
+
+            @pl.when(h != j)
+            def _():
+                wait_recv(y_full.at[chip, core, j], yh_r.at[j])
+
+        mine = y_half(i, chip, core)
+        for k in range(1, nc):
+            to = other_c(k)
+            send(mine, mine, yf_s.at[i, to], yf_r.at[i, chip], (to * 2 + core, h))
+        send(mine, mine, yw_s.at[i, chip], yw_r.at[i, chip], partner)
+
+    y_start(0)
+    value = tp_sum[h].astype(F32)
+    for k in range(1, nh):
+        fr = other_h(k)
+        wait_recv(tp_got.at[fr], th_r.at[fr])
+        value = value + tp_got[fr].astype(F32)
+    tq_sum[...] = value.astype(BF)
+    for k in range(1, nc):
+        to = other_c(k)
+        send(tq_sum.at[to], tq_got.at[chip], tf_s.at[to], tf_r.at[chip], (to * 2 + core, h))
 
     value = tq_sum[chip].astype(F32)
     for k in range(1, nc):
@@ -475,6 +498,7 @@
         to = other_c(k)
         here = tap_full.at[core, h, chip]
         send(here, here, tg_s.at[to], tg_r.at[chip], (to * 2 + core, h))
+    y_start(1)
     for k in range(1, nc):
         fr = other_c(k)
         wait_recv(tap_full.at[core, h, fr], tg_r.at[fr])
@@ -484,15 +508,32 @@
     send(tap_full.at[core, h], tap_full.at[core, h], tw_s.at[h], tw_r.at[h], partner)
 
     for k in range(1, nc):
+        to = other_c(k)
+        send(ra_full.at[chip, core], ra_full.at[chip, core], ff_s.at[to], ff_r.at[chip], (to * 2 + core, h))
+    send(ra_full.at[chip, core], ra_full.at[chip, core], fw_s.at[chip], fw_r.at[chip], partner)
+
+    for i in range(2):
+        for k in range(1, nc):
+            fr = other_c(k)
+            part = y_half(i, fr, core)
+            wait_recv(part, yf_r.at[i, fr])
+            send(part, part, yw_s.at[i, fr], yw_r.at[i, fr], partner)
+    for k in range(1, nc):
         fr = other_c(k)
-        wait_recv(y_full.at[fr, core], yf_r.at[fr])
-        send(y_full.at[fr, core], y_full.at[fr, core], yw_s.at[fr], yw_r.at[fr], partner)
+        wait_recv(ra_full.at[fr, core], ff_r.at[fr])
+        send(ra_full.at[fr, core], ra_full.at[fr, core], fw_s.at[fr], fw_r.at[fr], partner)
+
     for k in range(1, nh):
         fr = other_h(k)
         wait_recv(tap_full.at[core, fr], ta_r.at[fr])
         send(tap_full.at[core, fr], tap_full.at[core, fr], tw_s.at[fr], tw_r.at[fr], partner)
     for k in range(nc):
-        wait_recv(y_full.at[other_c(k), 1 - core], yw_r.at[other_c(k)])
+        wait_recv(ra_full.at[other_c(k), 1 - core], fw_r.at[other_c(k)])
+    push(3, ra_full, ra_o)
+
+    for i in range(2):
+        for k in range(nc):
+            wait_recv(y_half(i, other_c(k), 1 - core), yw_r.at[i, other_c(k)])
     push(4, y_full, y_o)
     for k in range(nh):
         wait_recv(tap_full.at[1 - core, other_h(k)], tw_r.at[other_h(k)])
@@ -524,17 +565,21 @@
         wait_send(tap_full.at[core, other_h(k)], tw_s.at[other_h(k)])
     wait_send(fp_pair, pair_s.at[0])
     wait_send(tp_pair, pair_s.at[1])
+    wait_send(xs_pair, pair_s.at[2])
     for k in range(1, nc):
         to = other_c(k)
         wait_send(fp_sum.at[to], fr_s.at[to])
+        wait_send(xs_sum.at[to], fx_s.at[to])
         wait_send(ra_full.at[chip, core], ff_s.at[to])
         wait_send(tq_sum.at[to], tf_s.at[to])
         wait_send(tap_full.at[core, h, chip], tg_s.at[to])
-        wait_send(y_full.at[chip, core], yf_s.at[to])
+        for i in range(2):
+            wait_send(y_half(i, chip, core), yf_s.at[i, to])
     for k in range(nc):
         to = other_c(k)
         wait_send(ra_full.at[to, core], fw_s.at[to])
-        wait_send(y_full.at[to, core], yw_s.at[to])
+        for i in range(2):
+            wait_send(y_half(i, to, core), yw_s.at[i, to])
     for j in range(z.na):
 
         @pl.when(h != j)
@@ -552,11 +597,11 @@
 
 
 def final_kernel(
-    z, ra_in, y_in, tap_in, w_aug_in, w_up_in, embed_col, out_in, gc_in,
+    z, ra_in, y_in, tap_in, w_aug_in, w_up_in, embed_row, out_in, gc_in,
     out_o, gc_o, time_o, down_o, embed_o, qkv_o, wout_o, up_o,
     ra, y, tap, w_aug, w_up, out, gc, time, down, emb, qkv, wout, up, in_s, out_s,
 ):
-    pulls = [(out_in, out), (gc_in, gc), (ra_in, ra), (w_aug_in, w_aug), (w_up_in, w_up), (y_in, y), (tap_in, tap)]
+    pulls = [(y_in, y), (tap_in, tap), (ra_in, ra), (w_aug_in, w_aug), (w_up_in, w_up), (out_in, out), (gc_in, gc)]
     pulls = [pltpu.make_async_copy(a, b, in_s.at[i]) for i, (a, b) in enumerate(pulls)]
     for pull in pulls:
         pull.start()
@@ -568,9 +613,16 @@
         pushes.append(copy)
 
     pulls[0].wait()
-    push(out, out_o)
+    grad_down = y[:, 0].astype(F32).reshape(CA, CC)
+    down[...] = grad_down[0:C]
+    push(down, down_o)
+    emb[...] = mm_t1(eye(C), jnp.broadcast_to(embed_row[...], (16, C)))[:, 0:1] * grad_down[C : C + 1]
+    push(emb, embed_o)
+    up[...] = y[:, 1].astype(F32).reshape(CA, CC)[0:C]
+    push(up, up_o)
     pulls[1].wait()
-    push(gc, gc_o)
+    time[...] = tap[...].astype(F32).reshape(1024, CA)[0:960, 0:C]
+    push(time, time_o)
     pulls[2].wait()
     pulls[3].wait()
     sums = flat(ra[...], RAW)
@@ -580,17 +632,9 @@
     wout[...] = mm_t0(sums[0:C, 480:RAW], w_up[...])
     push(wout, wout_o)
     pulls[5].wait()
-    both = y[...].astype(F32)
-    grad_down = both[:, 0].reshape(CA, CC)
-    down[...] = grad_down[0:C]
-    push(down, down_o)
-    emb[...] = embed_col[...] * grad_down[C : C + 1]
-    push(emb, embed_o)
-    up[...] = both[:, 1].reshape(CA, CC)[0:C]
-    push(up, up_o)
+    push(out, out_o)
     pulls[6].wait()
-    time[...] = tap[...].astype(F32).reshape(1024, CA)[0:960, 0:C]
-    push(time, time_o)
+    push(gc, gc_o)
     for copy in pushes:
         copy.wait()
 
@@ -598,7 +642,7 @@
 def shards(z, clip, w_time, w_down, w_embed, w_qkv, w_out, w_up, timestep, cotangent):
     nf, nh, nc = z.nf, z.nh, z.nc
     embed = time_embed(timestep, w_embed.shape[0])
-    embed_rows = jnp.broadcast_to(embed[None, :], (16, C))
+    embed_row = embed[None, :]
     vm = pl.BlockSpec(memory_space=pltpu.VMEM)
     hbm = pl.BlockSpec(memory_space=pl.ANY)
     dma = pltpu.SemaphoreType.DMA
@@ -633,24 +677,25 @@
             bf(nf, 8, CA), bf(nf, 8, CA), bf(nf, 8, CA), bf(nf, 8, CA),
             bf(nh, z.tok, CA), bf(nh, z.tok, CA), bf(nh * z.tok, 768), bf(nh * z.tok, 256),
             bf(nh, z.tok, LW), bf(nh, z.tok, LW), bf(nf, 8, CA), bf(nf, 8, CA),
-            bf(nc, 2, z.nr, 8, FPW), bf(nc, z.nr, 8, FPW), bf(nc, z.nr, 8, FPW), bf(nc, z.nr, 8, FPW),
+            bf(*ra_shape), bf(nc, z.nr, 8, RAW), bf(nc, z.nr, 8, RAW), bf(nc, z.nr, 8, RAW),
             bf(*tap_shape), bf(nh, nc, z.tr, CA), bf(nh, nc, z.tr, CA), bf(nh, nc, z.tr, CA),
             bf(nc, z.tr, CA), bf(nc, z.tr, CA),
-            bf(z.na, z.ns, 8, CC), bf(nh, z.ns, 8, CC), f32(z.na, z.ns, 8, CC),
-            dma((8,)), dma((6,)),
+            bf(z.na, z.ns, 8, CC), bf(nh, z.ns, 8, CC), f32(z.ns, 8, CC),
+            bf(nc, 2, z.nr, 8, CA), bf(nc, 2, z.ns, 8, CA), bf(nc, z.ns, 8, CA), bf(nc, z.ns, 8, CA), bf(nc, z.ns, 8, CA),
+            dma((8,)), dma((6,)), dma((nc,)), dma((nc,)),
             dma((2,)), dma((2,)), dma((2,)), dma((2,)),
             dma((2, nf)), dma((2, nf)), dma((2, nh)), dma((2, nh)),
             dma((nh,)), dma((nh,)), dma((nf,)), dma((nf,)),
-            dma((2,)), dma((2,)), dma((nc,)), dma((nc,)), dma((nc,)), dma((nc,)), dma((nc,)), dma((nc,)),
+            dma((3,)), dma((3,)), dma((nc,)), dma((nc,)), dma((nc,)), dma((nc,)), dma((nc,)), dma((nc,)),
             dma((nh,)), dma((nh,)), dma((nc,)), dma((nc,)), dma((nc,)), dma((nc,)),
             dma((nh,)), dma((nh,)), dma((nh,)), dma((nh,)),
-            dma((nh,)), dma((nh,)), dma((nh,)), dma((nh,)), dma((nc,)), dma((nc,)), dma((nc,)), dma((nc,)),
+            dma((nh,)), dma((nh,)), dma((nh,)), dma((nh,)), dma((2, nc)), dma((2, nc)), dma((2, nc)), dma((2, nc)),
         ],
         compiler_params=pltpu.CompilerParams(
             collective_id=0, has_side_effects=True, vmem_limit_bytes=60 * 1024 * 1024
         ),
     )(
-        jnp.swapaxes(clip, 2, 3), w_time, w_down, w_embed, w_qkv.T, w_out, w_up_t, embed_rows,
+        jnp.swapaxes(clip, 2, 3), w_time, w_down, w_embed, w_qkv.T, w_out, w_up_t, embed_row,
         jnp.swapaxes(cotangent, 2, 3),
     )
     out, grad_clip, ra_full, y_full, tap_full, w_aug = outs
@@ -669,7 +714,7 @@
         ],
         compiler_params=pltpu.CompilerParams(vmem_limit_bytes=60 * 1024 * 1024),
     )(
-        ra_full, y_full.reshape(nf, 2, z.nr, 8, CC), tap_full, w_aug, w_up_t, embed.astype(F32)[:, None],
+        ra_full, y_full.reshape(nf, 2, z.nr, 8, CC), tap_full, w_aug, w_up_t, embed_row,
         out, grad_clip,
     )
     out, grad_clip, grad_time, grad_down, grad_embed, grad_qkv, grad_out, grad_up = grads

time: 106 us -> 98.2 us (0.926)
  the two profiles are of different devices: /device:TPU:1 before, /device:TPU:3 now
where the time goes in v2:
time: 98.2 us; the launch traced here: 98.1 us
  Pallas kernels  95.9 us (98%)
  between operations  1.45 us (1%)
    pallas_call x1, Pallas kernels, shards(): pl.pallas_call(functools.partial(main_kernel, z), out_shape=(like(frames,...  89.2 us
    pallas_call x1, Pallas kernels, shards(): pl.pallas_call(functools.partial(final_kernel, z), out_shape=(like(frames...  6.75 us

profile of v2, /device:TPU:3, one launch (start us, length us, event | category | flops | bytes accessed | tf_op | source)
XLA Modules:
  0.0 98.1 jit_solution(15348432089130827735)
XLA Ops:
  1.3 0.7 fusion.embed.embed_row
  2.0 89.2 %shard_map.152 = (bf16[2,2,320,128]{3,2,1,0:T(8,128)(2,1)}, f32[2,2,320,128]{3,2,1,0:T(8,128)}, bf16[8,2,3,8,640]{4,3,2,1,0:T(8,128)(2,1)}, bf16[8,2,6,1,8,1280]...) custom-call(bf16[2,2,320,128]{3,2,1,0:T(8,128)(2,1)} %bitcast.17, ...), custom_call_target="tpu_custom_call" | custom-call | tf_op jit(solution)/shard_map/pallas_call | solution.py:663
  91.2 6.7 %shard_map.153 = (bf16[2,2,320,128]{3,2,1,0:T(8,128)(2,1)}, f32[2,2,320,128]{3,2,1,0:T(8,128)}, f32[960,320]{1,0:T(8,128)}, f32[320,1280]{1,0:T(8,128)}, f32[320...) custom-call(bf16[8,2,3,8,640]{4,3,2,1,0:T(8,128)(2,1)} %get-tuple-element.22.ra_in, ...), custom_call_target="tpu_custom_call" | custom-call | tf_op jit(solution)/shard_map/pallas_call | solution.py:702
  (1 shorter events, 0.0 us)

commit v3 on v2

--- a/solution.py
+++ b/solution.py
@@ -83,13 +83,13 @@
     ls_send, ls_got, slab_send, slab_got,
     fp, fp_pair, fp_sum, fp_got, tp, tp_pair, tp_sum, tp_got, tq_sum, tq_got,
     y_send, y_got, x_buf, x_all, xs, xs_pair, xs_sum, xs_got,
-    in_s, out_s, fx_s, fx_r,
+    in_s, out_s, fx_s, fx_r, yx_s, yx_r,
     halo_s, halo_r, hgs, hgr, a2a_s, a2a_r, ag_s, ag_r, rs_s, rs_r, sl_s, sl_r,
     pair_s, pair_r, fr_s, fr_r, ff_s, ff_r, fw_s, fw_r,
     th_s, th_r, tf_s, tf_r, tg_s, tg_r, ta_s, ta_r, tw_s, tw_r,
     ys_s, ys_r, yh_s, yh_r, yf_s, yf_r, yw_s, yw_r,
 ):
-    nf, nh, nc, nx = z.nf, z.nh, z.nc, z.nx
+    nf, nh, nc, nx, nz = z.nf, z.nh, z.nc, z.nx, z.nc // 2
     f, h = lax.axis_index("frames"), lax.axis_index("heads")
     chip, core = f // 2, lax.rem(f, 2)
     partner = (chip * 2 + 1 - core, h)
@@ -114,6 +114,15 @@
 
     def other_h(k):
         return lax.rem(h + k, nh)
+
+    def heads_out():
+        for off in ([2, nx - 1, 1, 0] if nx == 4 else range(nx)):
+            base = 2 * lax.rem(h // 2 + off, nx)
+            if off == 0:
+                yield base + 1 - lax.rem(h, 2)
+            else:
+                yield base + lax.rem(h, 2)
+                yield base + 1 - lax.rem(h, 2)
 
     def other_c(k):
         return lax.rem(chip + k, nc)
@@ -226,16 +235,14 @@
         fr = other_f(k)
         wait_recv(g_got.at[fr], a2a_r.at[0, fr])
     g_all[h] = mm(sel_g, flat(g_got[...], CA)).astype(BF)
-    for k in range(1, nh):
-        to = other_h(k)
+    for to in heads_out():
         send(g_all.at[h], g_all.at[h], ag_s.at[0, to], ag_r.at[0, h], (f, to))
 
     for k in range(1, nf):
         fr = other_f(k)
         wait_recv(p_got.at[fr], a2a_r.at[1, fr])
     p_all[h] = mm(sel_p, flat(p_got[...], CA)).astype(BF)
-    for k in range(1, nh):
-        to = other_h(k)
+    for to in heads_out():
         send(p_all.at[h], p_all.at[h], ag_s.at[1, to], ag_r.at[1, h], (f, to))
 
     bt = 2 * z.tok
@@ -247,41 +254,45 @@
         base = 2 * lax.rem(h // 2 + off, nx)
         return [mine] if off == 0 else [base, base + 1]
 
-    def block(off):
-        b = lax.rem(h // 2 + off, nx)
-        two = pl.ds(2 * b, 2)
-        rows = pl.ds(pl.multiple_of(b * bt, bt), bt)
-        pb = p_all[two].reshape(bt, CA)
-        gb = g_all[two].reshape(bt, CA)
+    def blocks(group):
+        where = [lax.rem(h // 2 + off, nx) for off in group]
+        twos = [pl.ds(2 * b, 2) for b in where]
+        pb = jnp.concatenate([p_all[two].reshape(bt, CA) for two in twos], axis=0)
+        gb = jnp.concatenate([g_all[two].reshape(bt, CA) for two in twos], axis=0)
         qkv = mm(pb, w2[...]).astype(BF)
         ag = mm_t1(gb, mh[...]).astype(BF)
-        grads, atts = [], []
-        for n in range(2):
-            q, k, v = (qkv[:, (3 * n + i) * 128 : (3 * n + i + 1) * 128] for i in range(3))
-            a = ag[:, n * 128 : (n + 1) * 128]
-            scores = jnp.where(mask, mm_t1(q, k) * SCALE, -1e30)
-            e = jnp.exp(scores - jnp.max(scores, axis=1, keepdims=True))
-            probs = e / jnp.sum(e, axis=1, keepdims=True)
-            weights = probs.astype(BF)
-            atts.append(mm(weights, v).astype(BF))
-            wg = mm_t1(a, v)
-            sg = (probs * (wg - jnp.sum(probs * wg, axis=1, keepdims=True)) * SCALE).astype(BF)
-            grads += [mm(sg, k).astype(BF), mm_t0(sg, q).astype(BF), mm_t0(weights, a).astype(BF)]
-        dg = jnp.concatenate(grads, axis=1)
-        att = jnp.concatenate(atts, axis=1)
-        dg_all[rows] = dg
-        att_all[rows] = att
-        ls_send[two] = (mm(att, mhl[...]) + mm_t1(dg, w2s[...])).astype(BF).reshape(2, z.tok, LW)
-
-    offs = [0, 1, 3, 2] if nx == 4 else list(range(nx))
-    for pair in [offs[i : i + 2] for i in range(0, nx, 2)]:
-        for off in pair:
+        dgs, atts = [], []
+        for i, b in enumerate(where):
+            grads, att = [], []
+            for n in range(2):
+                own = slice(i * bt, (i + 1) * bt)
+                q, k, v = (qkv[own, (3 * n + m) * 128 : (3 * n + m + 1) * 128] for m in range(3))
+                a = ag[own, n * 128 : (n + 1) * 128]
+                scores = jnp.where(mask, mm_t1(q, k) * SCALE, -1e30)
+                e = jnp.exp(scores - jnp.max(scores, axis=1, keepdims=True))
+                probs = e / jnp.sum(e, axis=1, keepdims=True)
+                weights = probs.astype(BF)
+                att.append(mm(weights, v).astype(BF))
+                wg = mm_t1(a, v)
+                sg = (probs * (wg - jnp.sum(probs * wg, axis=1, keepdims=True)) * SCALE).astype(BF)
+                grads += [mm(sg, k).astype(BF), mm_t0(sg, q).astype(BF), mm_t0(weights, a).astype(BF)]
+            dgs.append(jnp.concatenate(grads, axis=1))
+            atts.append(jnp.concatenate(att, axis=1))
+            rows = pl.ds(pl.multiple_of(b * bt, bt), bt)
+            dg_all[rows] = dgs[i]
+            att_all[rows] = atts[i]
+        dg, att = jnp.concatenate(dgs, axis=0), jnp.concatenate(atts, axis=0)
+        ls = (mm(att, mhl[...]) + mm_t1(dg, w2s[...])).astype(BF)
+        for i, two in enumerate(twos):
+            ls_send[two] = ls[i * bt : (i + 1) * bt].reshape(2, z.tok, LW)
+
+    for group in [[2, 1], [3, 0]] if nx == 4 else [list(range(nx))]:
+        for off in group:
             for fr in rows_needed(off):
                 wait_recv(g_all.at[fr], ag_r.at[0, fr])
                 wait_recv(p_all.at[fr], ag_r.at[1, fr])
-        for off in pair:
-            block(off)
-        for off in pair:
+        blocks(group)
+        for off in group:
             for to in rows_needed(off):
                 send(ls_send.at[to], ls_got.at[h], rs_s.at[to], rs_r.at[h], (f, to))
 
@@ -392,6 +403,11 @@
     tp[:, :, :, :, 0:C] = taps.reshape(2, nh, nc, z.tr, C).astype(BF)
     send(tp.at[1 - core], tp_pair, pair_s.at[1], pair_r.at[1], partner)
 
+    for k in range(1, nc):
+        to = other_c(k)
+        send(ra_full.at[chip, core], ra_full.at[chip, core], ff_s.at[to], ff_r.at[chip], (to * 2 + core, h))
+    send(ra_full.at[chip, core], ra_full.at[chip, core], fw_s.at[chip], fw_r.at[chip], partner)
+
     @pl.when(h < z.na)
     def _():
         xsum = xs_sum[chip].astype(F32)
@@ -461,23 +477,40 @@
             grad_clip[t, r] = acc[t, :, r * z.cols : (r + 1) * z.cols]
     push(2, grad_clip, gc_o)
 
+    zz, yy = chip // 2, lax.rem(chip, 2)
+    across = ((zz * 2 + 1 - yy) * 2 + core, h)
+
     def y_half(i, c, k):
-        return y_full.at[c, k, pl.ds(i * (z.na // 2), z.na // 2)]
-
-    def y_start(i):
-        for j in range(i * (z.na // 2), (i + 1) * (z.na // 2)):
-
-            @pl.when(h != j)
-            def _():
-                wait_recv(y_full.at[chip, core, j], yh_r.at[j])
-
-        mine = y_half(i, chip, core)
-        for k in range(1, nc):
-            to = other_c(k)
-            send(mine, mine, yf_s.at[i, to], yf_r.at[i, chip], (to * 2 + core, h))
-        send(mine, mine, yw_s.at[i, chip], yw_r.at[i, chip], partner)
-
-    y_start(0)
+        return y_full.at[pl.ds(2 * c, 2), k, pl.ds(i * (z.na // 2), z.na // 2)]
+
+    up_z, down_z = lax.rem(zz + 1, nz), lax.rem(zz + nz - 1, nz)
+
+    def y_send_z(i, c, to, slot):
+        part = y_half(i, c, core)
+        send(part, part, yf_s.at[i, slot], yf_r.at[i, c], ((to * 2 + yy) * 2 + core, h))
+
+    def y_pass(i, c):
+        part = y_half(i, c, core)
+        send(part, part, yw_s.at[i, c], yw_r.at[i, c], partner)
+
+    def y_start():
+        wait_recv(y_full.at[zz * 2 + 1 - yy, core], yx_r.at[0])
+        if nz > 1:
+            y_send_z(0, zz, up_z, 0)
+            y_send_z(1, zz, down_z, 0)
+            y_send_z(1, zz, up_z, 1)
+            y_send_z(0, zz, down_z, 1)
+        for i in range(2):
+            y_pass(i, zz)
+
+    for j in range(z.na):
+
+        @pl.when(h != j)
+        def _():
+            wait_recv(y_full.at[chip, core, j], yh_r.at[j])
+
+    send(y_full.at[chip, core], y_full.at[chip, core], yx_s.at[0], yx_r.at[0], across)
+
     value = tp_sum[h].astype(F32)
     for k in range(1, nh):
         fr = other_h(k)
@@ -498,7 +531,7 @@
         to = other_c(k)
         here = tap_full.at[core, h, chip]
         send(here, here, tg_s.at[to], tg_r.at[chip], (to * 2 + core, h))
-    y_start(1)
+    y_start()
     for k in range(1, nc):
         fr = other_c(k)
         wait_recv(tap_full.at[core, h, fr], tg_r.at[fr])
@@ -507,17 +540,21 @@
         send(tap_full.at[core, h], tap_full.at[core, h], ta_s.at[to], ta_r.at[h], (f, to))
     send(tap_full.at[core, h], tap_full.at[core, h], tw_s.at[h], tw_r.at[h], partner)
 
-    for k in range(1, nc):
-        to = other_c(k)
-        send(ra_full.at[chip, core], ra_full.at[chip, core], ff_s.at[to], ff_r.at[chip], (to * 2 + core, h))
-    send(ra_full.at[chip, core], ra_full.at[chip, core], fw_s.at[chip], fw_r.at[chip], partner)
-
-    for i in range(2):
-        for k in range(1, nc):
-            fr = other_c(k)
-            part = y_half(i, fr, core)
-            wait_recv(part, yf_r.at[i, fr])
-            send(part, part, yw_s.at[i, fr], yw_r.at[i, fr], partner)
+    if nz > 1:
+        far = lax.rem(zz + 2, nz)
+        wait_recv(y_half(0, down_z, core), yf_r.at[0, down_z])
+        y_send_z(0, down_z, up_z, 2)
+        wait_recv(y_half(1, up_z, core), yf_r.at[1, up_z])
+        y_send_z(1, up_z, down_z, 2)
+        y_pass(0, down_z)
+        y_pass(1, up_z)
+        wait_recv(y_half(1, down_z, core), yf_r.at[1, down_z])
+        y_pass(1, down_z)
+        wait_recv(y_half(0, up_z, core), yf_r.at[0, up_z])
+        y_pass(0, up_z)
+        for i in range(2):
+            wait_recv(y_half(i, far, core), yf_r.at[i, far])
+            y_pass(i, far)
     for k in range(1, nc):
         fr = other_c(k)
         wait_recv(ra_full.at[fr, core], ff_r.at[fr])
@@ -532,8 +569,9 @@
     push(3, ra_full, ra_o)
 
     for i in range(2):
-        for k in range(nc):
-            wait_recv(y_half(i, other_c(k), 1 - core), yw_r.at[i, other_c(k)])
+        for k in range(nz):
+            fr = lax.rem(zz + k, nz)
+            wait_recv(y_half(i, fr, 1 - core), yw_r.at[i, fr])
     push(4, y_full, y_o)
     for k in range(nh):
         wait_recv(tap_full.at[1 - core, other_h(k)], tw_r.at[other_h(k)])
@@ -573,13 +611,16 @@
         wait_send(ra_full.at[chip, core], ff_s.at[to])
         wait_send(tq_sum.at[to], tf_s.at[to])
         wait_send(tap_full.at[core, h, chip], tg_s.at[to])
-        for i in range(2):
-            wait_send(y_half(i, chip, core), yf_s.at[i, to])
     for k in range(nc):
         to = other_c(k)
         wait_send(ra_full.at[to, core], fw_s.at[to])
-        for i in range(2):
+    wait_send(y_full.at[chip, core], yx_s.at[0])
+    for i in range(2):
+        for k in range(nz):
+            to = lax.rem(zz + k, nz)
             wait_send(y_half(i, to, core), yw_s.at[i, to])
+        for slot in range(3 if nz > 1 else 0):
+            wait_send(y_half(i, zz, core), yf_s.at[i, slot])
     for j in range(z.na):
 
         @pl.when(h != j)
@@ -682,7 +723,7 @@
             bf(nc, z.tr, CA), bf(nc, z.tr, CA),
             bf(z.na, z.ns, 8, CC), bf(nh, z.ns, 8, CC), f32(z.ns, 8, CC),
             bf(nc, 2, z.nr, 8, CA), bf(nc, 2, z.ns, 8, CA), bf(nc, z.ns, 8, CA), bf(nc, z.ns, 8, CA), bf(nc, z.ns, 8, CA),
-            dma((8,)), dma((6,)), dma((nc,)), dma((nc,)),
+            dma((8,)), dma((6,)), dma((nc,)), dma((nc,)), dma((1,)), dma((1,)),
             dma((2,)), dma((2,)), dma((2,)), dma((2,)),
             dma((2, nf)), dma((2, nf)), dma((2, nh)), dma((2, nh)),
             dma((nh,)), dma((nh,)), dma((nf,)), dma((nf,)),

time: 98.2 us -> 92.7 us (0.944)
  the two profiles are of different devices: /device:TPU:3 before, /device:TPU:1 now
where the time goes in v3:
time: 92.7 us; the launch traced here: 92.5 us
  Pallas kernels  90.3 us (97%)
  between operations  1.45 us (2%)
    pallas_call x1, Pallas kernels, shards(): pl.pallas_call(functools.partial(main_kernel, z), out_shape=(like(frames,...  83.6 us
    pallas_call x1, Pallas kernels, shards(): pl.pallas_call(functools.partial(final_kernel, z), out_shape=(like(frames...  6.75 us

profile of v3, /device:TPU:1, one launch (start us, length us, event | category | flops | bytes accessed | tf_op | source)
XLA Modules:
  0.0 92.5 jit_solution(3026971323752966936)
XLA Ops:
  1.3 0.7 fusion.embed.embed_row
  2.0 83.6 %shard_map.152 = (bf16[2,2,320,128]{3,2,1,0:T(8,128)(2,1)}, f32[2,2,320,128]{3,2,1,0:T(8,128)}, bf16[8,2,3,8,640]{4,3,2,1,0:T(8,128)(2,1)}, bf16[8,2,6,1,8,1280]...) custom-call(bf16[2,2,320,128]{3,2,1,0:T(8,128)(2,1)} %bitcast.17, ...), custom_call_target="tpu_custom_call" | custom-call | tf_op jit(solution)/shard_map/pallas_call | solution.py:704
  85.6 6.7 %shard_map.153 = (bf16[2,2,320,128]{3,2,1,0:T(8,128)(2,1)}, f32[2,2,320,128]{3,2,1,0:T(8,128)}, f32[960,320]{1,0:T(8,128)}, f32[320,1280]{1,0:T(8,128)}, f32[320...) custom-call(bf16[8,2,3,8,640]{4,3,2,1,0:T(8,128)(2,1)} %get-tuple-element.22.ra_in, ...), custom_call_target="tpu_custom_call" | custom-call | tf_op jit(solution)/shard_map/pallas_call | solution.py:743
  (1 shorter events, 0.0 us)

commit v4 on v3

--- a/solution.py
+++ b/solution.py
@@ -74,16 +74,15 @@
 
 def main_kernel(
     z, clip_in, w_time_in, w_down_in, w_embed_in, w_qkv_in, w_out_in, w_up_in, embed, cot_in,
-    out_o, gc_o, ra_o, y_o, tap_o, w_aug_o,
+    out, grad_clip, ra_full, y_full, tap_full, w_aug,
     clip, w_time, w_down, w_embed, w_qkv, w_out, w_up, cot,
-    out, grad_clip, ra_full, y_full, tap_full, w_aug,
     clip_l, clip_r, hidden, hg, hg_l, hg_r, acc,
     w_t, w_qkvp, w2, w2s, mh, mhl, wdu,
     p_send, g_send, p_got, g_got, p_all, g_all, dg_all, att_all,
     ls_send, ls_got, slab_send, slab_got,
     fp, fp_pair, fp_sum, fp_got, tp, tp_pair, tp_sum, tp_got, tq_sum, tq_got,
     y_send, y_got, x_buf, x_all, xs, xs_pair, xs_sum, xs_got,
-    in_s, out_s, fx_s, fx_r, yx_s, yx_r,
+    in_s, fx_s, fx_r, yx_s, yx_r,
     halo_s, halo_r, hgs, hgr, a2a_s, a2a_r, ag_s, ag_r, rs_s, rs_r, sl_s, sl_r,
     pair_s, pair_r, fr_s, fr_r, ff_s, ff_r, fw_s, fw_r,
     th_s, th_r, tf_s, tf_r, tg_s, tg_r, ta_s, ta_r, tw_s, tw_r,
@@ -134,9 +133,6 @@
     pulls = [pltpu.make_async_copy(a, b, in_s.at[i]) for i, (a, b) in enumerate(pulls)]
     for pull in pulls:
         pull.start()
-
-    def push(i, src, dst):
-        pltpu.make_async_copy(src, dst, out_s.at[i]).start()
 
     barrier = pltpu.get_barrier_semaphore()
     for k in range(1, nf):
@@ -183,7 +179,6 @@
     shift = mm(jnp.broadcast_to(embed[...], (16, C)), w_embed[...])
     w_aug[0:C] = w_down[...]
     w_aug[C:CA] = jnp.where(iota((CA - C, CC), 0) == 0, jnp.broadcast_to(shift[0:1], (CA - C, CC)), 0.0).astype(BF)
-    push(0, w_aug, w_aug_o)
     w_qkvp[...] = jnp.zeros_like(w_qkvp)
     for i in range(6):
         w_qkvp[128 * i : 128 * i + HD] = w_qkv[HD * i : HD * i + HD]
@@ -452,7 +447,6 @@
         value = (hidden[t].astype(F32) + lifted).astype(BF)
         for r in range(2):
             out[t, r] = value[:, r * z.cols : (r + 1) * z.cols]
-    push(1, out, out_o)
 
     @pl.when(f > 0)
     def _():
@@ -475,7 +469,6 @@
     for t in range(2):
         for r in range(2):
             grad_clip[t, r] = acc[t, :, r * z.cols : (r + 1) * z.cols]
-    push(2, grad_clip, gc_o)
 
     zz, yy = chip // 2, lax.rem(chip, 2)
     across = ((zz * 2 + 1 - yy) * 2 + core, h)
@@ -566,16 +559,13 @@
         send(tap_full.at[core, fr], tap_full.at[core, fr], tw_s.at[fr], tw_r.at[fr], partner)
     for k in range(nc):
         wait_recv(ra_full.at[other_c(k), 1 - core], fw_r.at[other_c(k)])
-    push(3, ra_full, ra_o)
 
     for i in range(2):
         for k in range(nz):
             fr = lax.rem(zz + k, nz)
             wait_recv(y_half(i, fr, 1 - core), yw_r.at[i, fr])
-    push(4, y_full, y_o)
     for k in range(nh):
         wait_recv(tap_full.at[1 - core, other_h(k)], tw_r.at[other_h(k)])
-    push(5, tap_full, tap_o)
 
     @pl.when(f > 0)
     def _():
@@ -632,20 +622,14 @@
         for k in range(1, nh):
             wait_send(y_full.at[chip, core, h], yh_s.at[other_h(k)])
 
-    pushes = [(w_aug, w_aug_o), (out, out_o), (grad_clip, gc_o), (ra_full, ra_o), (y_full, y_o), (tap_full, tap_o)]
-    for i, (a, b) in enumerate(pushes):
-        pltpu.make_async_copy(a, b, out_s.at[i]).wait()
-
 
 def final_kernel(
-    z, ra_in, y_in, tap_in, w_aug_in, w_up_in, embed_row, out_in, gc_in,
+    z, ra, y, tap, w_aug, w_up_in, embed_row, out, gc,
     out_o, gc_o, time_o, down_o, embed_o, qkv_o, wout_o, up_o,
-    ra, y, tap, w_aug, w_up, out, gc, time, down, emb, qkv, wout, up, in_s, out_s,
+    w_up, time, down, emb, qkv, wout, up, in_s, out_s,
 ):
-    pulls = [(y_in, y), (tap_in, tap), (ra_in, ra), (w_aug_in, w_aug), (w_up_in, w_up), (out_in, out), (gc_in, gc)]
-    pulls = [pltpu.make_async_copy(a, b, in_s.at[i]) for i, (a, b) in enumerate(pulls)]
-    for pull in pulls:
-        pull.start()
+    pull = pltpu.make_async_copy(w_up_in, w_up, in_s.at[0])
+    pull.start()
     pushes = []
 
     def push(src, dst):
@@ -653,7 +637,8 @@
         copy.start()
         pushes.append(copy)
 
-    pulls[0].wait()
+    push(gc, gc_o)
+    push(out, out_o)
     grad_down = y[:, 0].astype(F32).reshape(CA, CC)
     down[...] = grad_down[0:C]
     push(down, down_o)
@@ -661,21 +646,14 @@
     push(emb, embed_o)
     up[...] = y[:, 1].astype(F32).reshape(CA, CC)[0:C]
     push(up, up_o)
-    pulls[1].wait()
     time[...] = tap[...].astype(F32).reshape(1024, CA)[0:960, 0:C]
     push(time, time_o)
-    pulls[2].wait()
-    pulls[3].wait()
     sums = flat(ra[...], RAW)
     qkv[...] = mm_t0(sums[:, 0:480], w_aug[...])
     push(qkv, qkv_o)
-    pulls[4].wait()
+    pull.wait()
     wout[...] = mm_t0(sums[0:C, 480:RAW], w_up[...])
     push(wout, wout_o)
-    pulls[5].wait()
-    push(out, out_o)
-    pulls[6].wait()
-    push(gc, gc_o)
     for copy in pushes:
         copy.wait()
 
@@ -685,7 +663,7 @@
     embed = time_embed(timestep, w_embed.shape[0])
     embed_row = embed[None, :]
     vm = pl.BlockSpec(memory_space=pltpu.VMEM)
-    hbm = pl.BlockSpec(memory_space=pl.ANY)
+    hbm = pl.BlockSpec(memory_space=pltpu.HBM)
     dma = pltpu.SemaphoreType.DMA
 
     def bf(*shape):
@@ -693,6 +671,9 @@
 
     def f32(*shape):
         return pltpu.VMEM(shape, F32)
+
+    def far(x):
+        return pltpu.with_memory_space_constraint(x, pltpu.HBM)
 
     def like(kind, dtype):
         return jax.ShapeDtypeStruct(kind, dtype)
@@ -708,10 +689,9 @@
             like(tap_shape, BF), like((CA, CC), BF),
         ),
         in_specs=[hbm] * 7 + [vm, hbm],
-        out_specs=(hbm,) * 6,
+        out_specs=(vm,) * 6,
         scratch_shapes=[
             bf(*frames), bf(3, C, C), bf(C, CC), bf(C, CC), bf(480, CC), bf(2 * HD, CC), bf(C, CC), bf(*frames),
-            bf(*frames), f32(*frames), bf(*ra_shape), bf(*y_shape), bf(*tap_shape), bf(CA, CC),
             bf(*frames[1:]), bf(*frames[1:]), bf(2, C, z.cells), bf(*frames), bf(*frames[1:]), bf(*frames[1:]),
             f32(2, C, z.cells),
             bf(3, C, C), bf(768, CC), bf(CA, 768), bf(LW, 768), bf(256, CA), bf(256, LW), bf(CA, CA),
@@ -723,7 +703,7 @@
             bf(nc, z.tr, CA), bf(nc, z.tr, CA),
             bf(z.na, z.ns, 8, CC), bf(nh, z.ns, 8, CC), f32(z.ns, 8, CC),
             bf(nc, 2, z.nr, 8, CA), bf(nc, 2, z.ns, 8, CA), bf(nc, z.ns, 8, CA), bf(nc, z.ns, 8, CA), bf(nc, z.ns, 8, CA),
-            dma((8,)), dma((6,)), dma((nc,)), dma((nc,)), dma((1,)), dma((1,)),
+            dma((8,)), dma((nc,)), dma((nc,)), dma((1,)), dma((1,)),
             dma((2,)), dma((2,)), dma((2,)), dma((2,)),
             dma((2, nf)), dma((2, nf)), dma((2, nh)), dma((2, nh)),
             dma((nh,)), dma((nh,)), dma((nf,)), dma((nf,)),
@@ -733,11 +713,11 @@
             dma((nh,)), dma((nh,)), dma((nh,)), dma((nh,)), dma((2, nc)), dma((2, nc)), dma((2, nc)), dma((2, nc)),
         ],
         compiler_params=pltpu.CompilerParams(
-            collective_id=0, has_side_effects=True, vmem_limit_bytes=60 * 1024 * 1024
+            collective_id=0, has_side_effects=True, vmem_limit_bytes=36 * 1024 * 1024
         ),
     )(
-        jnp.swapaxes(clip, 2, 3), w_time, w_down, w_embed, w_qkv.T, w_out, w_up_t, embed_row,
-        jnp.swapaxes(cotangent, 2, 3),
+        far(jnp.swapaxes(clip, 2, 3)), far(w_time), far(w_down), far(w_embed), far(w_qkv.T), far(w_out),
+        far(w_up_t), embed_row, far(jnp.swapaxes(cotangent, 2, 3)),
     )
     out, grad_clip, ra_full, y_full, tap_full, w_aug = outs
     grads = pl.pallas_call(
@@ -746,16 +726,16 @@
             like(frames, BF), like(frames, F32), like((960, C), F32), like((C, CC), F32), like((C, CC), F32),
             like((480, CC), F32), like((2 * HD, CC), F32), like((C, CC), F32),
         ),
-        in_specs=[hbm] * 5 + [vm, hbm, hbm],
+        in_specs=[vm] * 4 + [hbm, vm, vm, vm],
         out_specs=(hbm,) * 8,
         scratch_shapes=[
-            bf(*ra_shape), bf(nf, 2, z.nr, 8, CC), bf(*tap_shape), bf(CA, CC), bf(C, CC), bf(*frames), f32(*frames),
+            bf(C, CC),
             f32(960, C), f32(C, CC), f32(C, CC), f32(480, CC), f32(2 * HD, CC), f32(C, CC),
-            dma((7,)), dma((8,)),
+            dma((1,)), dma((8,)),
         ],
-        compiler_params=pltpu.CompilerParams(vmem_limit_bytes=60 * 1024 * 1024),
+        compiler_params=pltpu.CompilerParams(vmem_limit_bytes=36 * 1024 * 1024),
     )(
-        ra_full, y_full.reshape(nf, 2, z.nr, 8, CC), tap_full, w_aug, w_up_t, embed_row,
+        ra_full, y_full.reshape(nf, 2, z.nr, 8, CC), tap_full, w_aug, far(w_up_t), embed_row,
         out, grad_clip,
     )
     out, grad_clip, grad_time, grad_down, grad_embed, grad_qkv, grad_out, grad_up = grads

time: 92.7 us -> 89 us (0.960)
  Pallas kernels: 90.3 us -> 87.3 us
    pallas_call x1, Pallas kernels: 6.75 us -> 4.79 us  [shards(): pl.pallas_call(functools.partial(final_kernel, z), out_shape=(like(frames...]
    pallas_call x1, Pallas kernels: 83.6 us -> 82.5 us  [shards(): pl.pallas_call(functools.partial(main_kernel, z), out_shape=(like(frames,...]
where the time goes in v4:
time: 89 us; the launch traced here: 88.8 us
  Pallas kernels  87.3 us (98%)
  between operations  1.45 us (2%)
    pallas_call x1, Pallas kernels, shards(): pl.pallas_call(functools.partial(main_kernel, z), out_shape=(like(frames,...  82.5 us
    pallas_call x1, Pallas kernels, shards(): pl.pallas_call(functools.partial(final_kernel, z), out_shape=(like(frames...  4.79 us

profile of v4, /device:TPU:1, one launch (start us, length us, event | category | flops | bytes accessed | tf_op | source)
XLA Modules:
  0.0 88.8 jit_solution(7082946149247890407)
XLA Ops:
  1.3 0.1 fusion.embed.embed_row
  1.4 82.5 %shard_map.152 = (bf16[2,2,320,128]{3,2,1,0:T(8,128)(2,1)S(1)}, f32[2,2,320,128]{3,2,1,0:T(8,128)S(1)}, bf16[8,2,3,8,640]{4,3,2,1,0:T(8,128)(2,1)S(1)}, bf16[8,2...) custom-call(bf16[2,2,320,128]{3,2,1,0:T(8,128)(2,1)} %bitcast.17, ...), custom_call_target="tpu_custom_call" | custom-call | tf_op jit(solution)/shard_map/pallas_call | solution.py:685
  83.9 4.8 %shard_map.153 = (bf16[2,2,320,128]{3,2,1,0:T(8,128)(2,1)}, f32[2,2,320,128]{3,2,1,0:T(8,128)}, f32[960,320]{1,0:T(8,128)}, f32[320,1280]{1,0:T(8,128)}, f32[320...) custom-call(bf16[8,2,3,8,640]{4,3,2,1,0:T(8,128)(2,1)S(1)} %get-tuple-element.22.ra, ...), custom_call_target="tpu_custom_call" | custom-call | tf_op jit(solution)/shard_map/pallas_call | solution.py:723
  (1 shorter events, 0.0 us)

commit v5 on v4

--- a/solution.py
+++ b/solution.py
@@ -233,6 +233,7 @@
     for to in heads_out():
         send(g_all.at[h], g_all.at[h], ag_s.at[0, to], ag_r.at[0, h], (f, to))
 
+    tp[...] = jnp.zeros_like(tp)
     for k in range(1, nf):
         fr = other_f(k)
         wait_recv(p_got.at[fr], a2a_r.at[1, fr])
@@ -281,7 +282,7 @@
         for i, two in enumerate(twos):
             ls_send[two] = ls[i * bt : (i + 1) * bt].reshape(2, z.tok, LW)
 
-    for group in [[2, 1], [3, 0]] if nx == 4 else [list(range(nx))]:
+    for group in [[2], [1], [3, 0]] if nx == 4 else [list(range(nx))]:
         for off in group:
             for fr in rows_needed(off):
                 wait_recv(g_all.at[fr], ag_r.at[0, fr])
@@ -394,7 +395,6 @@
         ],
         axis=0,
     )
-    tp[...] = jnp.zeros_like(tp)
     tp[:, :, :, :, 0:C] = taps.reshape(2, nh, nc, z.tr, C).astype(BF)
     send(tp.at[1 - core], tp_pair, pair_s.at[1], pair_r.at[1], partner)
 

time: 89 us -> 87 us (0.978)
  Pallas kernels: 87.3 us -> 85.3 us
    pallas_call x1, Pallas kernels: 82.5 us -> 80.5 us  [shards(): pl.pallas_call(functools.partial(main_kernel, z), out_shape=(like(frames,...]
where the time goes in v5:
time: 87 us; the launch traced here: 86.9 us
  Pallas kernels  85.3 us (98%)
  between operations  1.45 us (2%)
    pallas_call x1, Pallas kernels, shards(): pl.pallas_call(functools.partial(main_kernel, z), out_shape=(like(frames,...  80.5 us
    pallas_call x1, Pallas kernels, shards(): pl.pallas_call(functools.partial(final_kernel, z), out_shape=(like(frames...  4.79 us

profile of v5, /device:TPU:1, one launch (start us, length us, event | category | flops | bytes accessed | tf_op | source)
XLA Modules:
  0.0 86.9 jit_solution(12217264730626215764)
XLA Ops:
  1.3 0.1 fusion.embed.embed_row
  1.4 80.5 %shard_map.152 = (bf16[2,2,320,128]{3,2,1,0:T(8,128)(2,1)S(1)}, f32[2,2,320,128]{3,2,1,0:T(8,128)S(1)}, bf16[8,2,3,8,640]{4,3,2,1,0:T(8,128)(2,1)S(1)}, bf16[8,2...) custom-call(bf16[2,2,320,128]{3,2,1,0:T(8,128)(2,1)} %bitcast.17, ...), custom_call_target="tpu_custom_call" | custom-call | tf_op jit(solution)/shard_map/pallas_call | solution.py:685
  81.9 4.8 %shard_map.153 = (bf16[2,2,320,128]{3,2,1,0:T(8,128)(2,1)}, f32[2,2,320,128]{3,2,1,0:T(8,128)}, f32[960,320]{1,0:T(8,128)}, f32[320,1280]{1,0:T(8,128)}, f32[320...) custom-call(bf16[8,2,3,8,640]{4,3,2,1,0:T(8,128)(2,1)S(1)} %get-tuple-element.22.ra, ...), custom_call_target="tpu_custom_call" | custom-call | tf_op jit(solution)/shard_map/pallas_call | solution.py:723
  (1 shorter events, 0.0 us)
